TPU v7x, 128 devices: a whole 4x4x4 slice. The times are simulated.
128 devices in a mesh: dom: 128 (over z, y, x, core).
Axes of the slice: x: 4, y: 4, z: 4, core: 2. Of those that a mesh axis runs over, the one named last changes fastest.
Arguments:
- right_side: float32 [18, 131072], P(None, 'dom'), may hold values from -20 to 20
- element_matrix: bfloat16 [72, 72, 65536], P(None, None, 'dom'), may hold values from -8 to 8, as said below
- face_map: int32 [4, 65536], P(None, 'dom'), may hold values from 0 to 1535
- share_index: int32 [128, 4, 128], P('dom'), may hold values from 0 to 1023
- share_count: int32 [128, 4], P('dom'), may hold values from 0 to 128, as said below
- face_mass: float32 [131072], P('dom'), may hold values from 0.5 to 2
- absorbing: int32 [131072], P('dom'), may hold values 0 or 1
- impedance: float32 [131072], P('dom'), may hold values from 0.5 to 4
Outputs:
- solution: float32 [18, 131072], P(None, 'dom')
- residual: float32 [18, 131072], P(None, 'dom')
Inputs may be any that keep to these rules, and one draw needn't show every extreme that they name: `element_matrix`: each element's 72 x 72 matrix is symmetric positive definite. share_count[d, k] is 0 where device d + o_k lies outside the axis; it equals 128 for some device and offset in every draw.
All inputs are finite; a program needn't handle non-finite values. No bound on the sum of `absorbing` on one device may be relied on, other than what follows from the above.
Results may differ from a plain program's by a relative error of at most 0.0003.
Values sent between devices are 32-bit elements; how exact they have to be, the bound alone decides.
A program may use at most 64 MiB of HBM per device.

v0:
```python
import functools

import jax
import jax.numpy as jnp
from jax import lax
from jax.sharding import Mesh
from jax.sharding import PartitionSpec as P

ITERS = 2
DOM = ("dom_0", "dom_1", "dom_2", "dom_3")


def passed_along(value, axis, steps):
    count = lax.axis_size(axis)
    first, last = (max(0, -steps), min(count, count - steps))
    return lax.ppermute(value, axis, [(source, source + steps) for source in range(first, last)])


def by_axis(value, axes):
    return functools.reduce(lax.psum, axes, value)


def offset_list(block_count):
    half_count = block_count // 2
    return [
        block_index - half_count if block_index < half_count else block_index - half_count + 1
        for block_index in range(block_count)
    ]


def shards(
    right_side, element_matrix, face_map, share_index, share_count, face_mass, absorbing, impedance
):
    trace_width = right_side.shape[0]
    own_faces = right_side.shape[1]
    side_count = face_map.shape[0]
    element_count = face_map.shape[1]
    block_count = share_index.shape[1]
    block_width = share_index.shape[2]
    dof_count = side_count * trace_width
    slot_total = own_faces + block_count * block_width
    offsets = offset_list(block_count)
    send_rows = share_index[0]
    slot_iota = lax.broadcasted_iota(jnp.int32, (block_count, block_width), 1)
    alive_mask = (slot_iota < share_count[0][:, None]).astype(jnp.float32)
    diagonal = face_mass + absorbing.astype(jnp.float32) * impedance
    flat_map = face_map.reshape(side_count * element_count)
    selector = (
        lax.broadcasted_iota(jnp.int32, (slot_total, side_count * element_count), 0)
        == flat_map[None, :]
    ).astype(jnp.float32)

    def fetch_ghosts(outgoing):
        received = []
        for block_index in range(block_count):
            received.append(passed_along(outgoing[block_index], DOM, offsets[block_index]))
        return jnp.stack(received)

    def return_sums(partial_value):
        received = []
        for block_index in range(block_count):
            received.append(passed_along(partial_value[block_index], DOM, -offsets[block_index]))
        return jnp.stack(received)

    def operate(field_now):
        outgoing = (
            jnp.take(field_now, send_rows, axis=1).transpose(1, 0, 2) * alive_mask[:, None, :]
        )
        ghosts = fetch_ghosts(outgoing)
        extended = jnp.concatenate(
            [field_now, ghosts.transpose(1, 0, 2).reshape(trace_width, block_count * block_width)],
            axis=1,
        )
        gathered = jnp.dot(
            extended, selector, precision=lax.Precision.HIGHEST, preferred_element_type=jnp.float32
        )
        picked = (
            gathered.reshape(trace_width, side_count, element_count)
            .transpose(1, 0, 2)
            .reshape(dof_count, element_count)
        )
        product = jnp.sum(element_matrix.astype(jnp.float32) * picked[None, :, :], axis=1)
        spread = (
            product.reshape(side_count, trace_width, element_count)
            .transpose(1, 0, 2)
            .reshape(trace_width, side_count * element_count)
        )
        summed = lax.dot_general(
            spread,
            selector,
            (((1,), (1,)), ((), ())),
            precision=lax.Precision.HIGHEST,
            preferred_element_type=jnp.float32,
        )
        partial_value = (
            summed[:, own_faces:].reshape(trace_width, block_count, block_width).transpose(1, 0, 2)
        )
        returned = return_sums(partial_value) * alive_mask[:, None, :]
        result = summed[:, :own_faces].at[:, send_rows].add(returned.transpose(1, 0, 2))
        return result + diagonal[None, :] * field_now

    def paired(values, image_vec):
        return (by_axis(jnp.sum(values * values), DOM), by_axis(jnp.sum(values * image_vec), DOM))

    solution = jnp.zeros_like(right_side)
    residual = right_side
    image_vec = operate(residual)
    norm_now, curvature = paired(residual, image_vec)
    step_size = norm_now / curvature
    direction = residual
    image_dir = image_vec
    for rounds in range(ITERS):
        solution = solution + step_size * direction
        residual = residual - step_size * image_dir
        if rounds + 1 < ITERS:
            image_vec = operate(residual)
            norm_next, curvature = paired(residual, image_vec)
            beta_ratio = norm_next / norm_now
            step_size = norm_next / (curvature - beta_ratio * norm_next / step_size)
            direction = residual + beta_ratio * direction
            image_dir = image_vec + beta_ratio * image_dir
            norm_now = norm_next
    return (solution, residual)


def solution(mesh):
    torus = Mesh(mesh.devices.reshape(4, 4, 4, 2), ("dom_0", "dom_1", "dom_2", "dom_3"))
    in_specs = (
        P(None, DOM),
        P(None, None, DOM),
        P(None, DOM),
        P(DOM, None, None),
        P(DOM, None),
        P(DOM),
        P(DOM),
        P(DOM),
    )
    out_specs = (P(None, DOM), P(None, DOM))
    return jax.shard_map(
        shards, mesh=torus, in_specs=in_specs, out_specs=out_specs, check_vma=False
    )
```

profile of v0, /device:TPU:1, one launch (start us, length us, event | category | flops | bytes accessed | tf_op | source)
XLA Modules:
  0.0 202.6 jit_solution(18133817289970364441)
XLA Ops:
  5.7 4.6 %collective-permute-start.3 = (f32[18,128]{1,0:T(8,128)S(1)}, f32[18,128]{1,0:T(8,128)S(1)}, u32[]{:S(2)}, u32[]{:S(2)}) collective-permute-start(f32[18,128]{1,0:T(8,128)S(1)} %get-tuple-element.34), channel_id=1, source_target_pairs={{0,2},{1,3},{2,4},{3,5},{4,6},{5,7},{6,8},{7,9},{8,10},{9,11},{10,... | collective-permute-start | bytes 27656 | tf_op jit(solution)/shard_map/ppermute | solution.py:16
  10.3 4.5 %collective-permute-start.2 = (f32[18,128]{1,0:T(8,128)S(1)}, f32[18,128]{1,0:T(8,128)S(1)}, u32[]{:S(2)}, u32[]{:S(2)}) collective-permute-start(f32[18,128]{1,0:T(8,128)S(1)} %get-tuple-element.35), channel_id=1, source_target_pairs={{0,1},{1,2},{2,3},{3,4},{4,5},{5,6},{6,7},{7,8},{8,9},{9,10},{10,1... | collective-permute-start | bytes 27656 | tf_op jit(solution)/shard_map/ppermute | solution.py:16
  19.8 4.9 %fusion.3 = f32[18,2048]{1,0:T(8,128)S(1)} fusion(s32[2048]{0:T(1024)S(1)} %bitcast.155, f32[18,512]{1,0:T(8,128)S(1)} %bitcast.133, f32[18,1024]{1,0:T(8,128)} %param.10), kind=kOutput, calls=%fused_computation.10 | convolution fusion | flops 682650624 | bytes 266240 | tf_op jit(solution)/shard_map/dot_general | solution.py:74
  25.0 4.1 %fusion.4 = f32[72,512]{1,0:T(8,128)S(1)} fusion(bf16[72,72,512]{2,1,0:T(8,128)(2,1)} %param.11, f32[72,512]{1,0:T(8,128)S(1)} %mul.120), kind=kLoop, calls=%fused_computation.11 | loop fusion | flops 7925760 | bytes 5603328 | tf_op jit(solution)/shard_map/reduce_sum | solution.py:82
  29.3 5.6 %fusion.2 = f32[18,1536]{1,0:T(8,128)S(1)} fusion(f32[18,2048]{1,0:T(8,128)S(1)} %bitcast.128, s32[2048]{0:T(1024)S(1)} %bitcast.156), kind=kOutput, calls=%fused_computation.9 | convolution fusion | flops 682622976 | bytes 266240 | tf_op jit(solution)/shard_map/dot_general | solution.py:88
  38.2 4.3 %collective-permute-start.5 = (f32[18,128]{1,0:T(8,128)S(1)}, f32[18,128]{1,0:T(8,128)S(1)}, u32[]{:S(2)}, u32[]{:S(2)}) collective-permute-start(f32[18,128]{1,0:T(8,128)S(1)} %bitcast.148), channel_id=1, source_target_pairs={{0,1},{1,2},{2,3},{3,4},{4,5},{5,6},{6,7},{7,8},{8,9},{9,10},{10,1... | collective-permute-start | bytes 27656 | tf_op jit(solution)/shard_map/ppermute | solution.py:16
  42.5 3.6 %collective-permute-start.4 = (f32[18,128]{1,0:T(8,128)S(1)}, f32[18,128]{1,0:T(8,128)S(1)}, u32[]{:S(2)}, u32[]{:S(2)}) collective-permute-start(f32[18,128]{1,0:T(8,128)S(1)} %bitcast.147), channel_id=1, source_target_pairs={{0,2},{1,3},{2,4},{3,5},{4,6},{5,7},{6,8},{7,9},{8,10},{9,11},{10,... | collective-permute-start | bytes 27656 | tf_op jit(solution)/shard_map/ppermute | solution.py:16
  47.2 3.7 %scatter_fusion = f32[18,1024]{0,1:T(8,128)S(1)} fusion(f32[18,1024]{0,1:T(8,128)S(1)} %copy.40, s32[512]{0:T(512)S(1)} %fusion.20, f32[512,18]{1,0:T(8,128)S(1)} %bitcast.124), kind=kCustom, calls=%fused_computation.2 | custom fusion | flops 9216 | bytes 112640 | tf_op jit(solution)/shard_map/scatter-add | solution.py:99
  51.8 26.5 %all-reduce.5 = (f32[]{:T(128)}, f32[]{:T(128)}) all-reduce(f32[]{:T(128)} %get-tuple-element.23, f32[]{:T(128)} %multiply_reduce_fusion), channel_id=1, replica_groups=mesh['dom_0'=4,'dom_1'=4,'dom_2'=4,'dom_3'=2] {'dom_0'}, use_global_device_ids=true, to_apply=%region_1.2 | all-reduce | flops 2 | bytes 16 | tf_op jit(solution)/shard_map/psum | solution.py:20
  78.3 6.6 %all-reduce.3 = (f32[]{:T(128)}, f32[]{:T(128)}) all-reduce(f32[]{:T(128)} %get-tuple-element.15, f32[]{:T(128)} %get-tuple-element.16), channel_id=1, replica_groups=mesh['dom_0'=4,'dom_1'=4,'dom_2'=4,'dom_3'=2] {'dom_1'}, use_global_device_ids=true, to_apply=%region_2.3 | all-reduce | flops 2 | bytes 16 | tf_op jit(solution)/shard_map/psum | solution.py:20
  84.9 6.6 %all-reduce.1 = (f32[]{:T(128)}, f32[]{:T(128)}) all-reduce(f32[]{:T(128)} %get-tuple-element.11, f32[]{:T(128)} %get-tuple-element.12), channel_id=1, replica_groups=mesh['dom_0'=4,'dom_1'=4,'dom_2'=4,'dom_3'=2] {'dom_2'}, use_global_device_ids=true, to_apply=%region_3.4 | all-reduce | flops 2 | bytes 16 | tf_op jit(solution)/shard_map/psum | solution.py:20
  91.6 7.9 %all-reduce.7 = (f32[]{:T(128)}, f32[]{:T(128)}) all-reduce(f32[]{:T(128)} %get-tuple-element.7, f32[]{:T(128)} %get-tuple-element.8), channel_id=1, replica_groups=mesh['dom_0'=4,'dom_1'=4,'dom_2'=4,'dom_3'=2] {'dom_3'}, use_global_device_ids=true, to_apply=%region_4.5 | all-reduce | flops 2 | bytes 16 | tf_op jit(solution)/shard_map/psum | solution.py:20
  103.5 4.5 %collective-permute-start.10 = (f32[18,128]{1,0:T(8,128)S(1)}, f32[18,128]{1,0:T(8,128)S(1)}, u32[]{:S(2)}, u32[]{:S(2)}) collective-permute-start(f32[18,128]{1,0:T(8,128)S(1)} %get-tuple-element.31), channel_id=1, source_target_pairs={{0,1},{1,2},{2,3},{3,4},{4,5},{5,6},{6,7},{7,8},{8,9},{9,10},{10,1... | collective-permute-start | bytes 27656 | tf_op jit(solution)/shard_map/ppermute | solution.py:16
  109.9 3.6 %collective-permute-start.11 = (f32[18,128]{1,0:T(8,128)S(1)}, f32[18,128]{1,0:T(8,128)S(1)}, u32[]{:S(2)}, u32[]{:S(2)}) collective-permute-start(f32[18,128]{1,0:T(8,128)S(1)} %get-tuple-element.30), channel_id=1, source_target_pairs={{0,2},{1,3},{2,4},{3,5},{4,6},{5,7},{6,8},{7,9},{8,10},{9,11},{10,... | collective-permute-start | bytes 27656 | tf_op jit(solution)/shard_map/ppermute | solution.py:16
  114.5 4.0 %fusion.1 = f32[18,2048]{1,0:T(8,128)S(1)} fusion(s32[2048]{0:T(1024)S(1)} %bitcast.157, f32[18,512]{1,0:T(8,128)S(1)} %bitcast.134, f32[18,1024]{1,0:T(8,128)S(1)} %multiply_subtract_fusion.1), kind=kOutput, calls=%fused_computation.8 | convolution fusion | flops 682650624 | bytes 266240 | tf_op jit(solution)/shard_map/dot_general | solution.py:74
  118.7 4.0 %fusion.5 = f32[72,512]{1,0:T(8,128)S(1)} fusion(bf16[72,72,512]{2,1,0:T(8,128)(2,1)} %param.11, f32[72,512]{1,0:T(8,128)S(1)} %mul.135), kind=kLoop, calls=%fused_computation.12 | loop fusion | flops 7925760 | bytes 5603328 | tf_op jit(solution)/shard_map/reduce_sum | solution.py:82
  123.0 5.6 %fusion = f32[18,1536]{1,0:T(8,128)S(1)} fusion(f32[18,2048]{1,0:T(8,128)S(1)} %bitcast.127, s32[2048]{0:T(1024)S(1)} %bitcast.158), kind=kOutput, calls=%fused_computation.7 | convolution fusion | flops 682622976 | bytes 266240 | tf_op jit(solution)/shard_map/dot_general | solution.py:88
  128.7 3.6 %collective-permute-start.12 = (f32[18,128]{1,0:T(8,128)S(1)}, f32[18,128]{1,0:T(8,128)S(1)}, u32[]{:S(2)}, u32[]{:S(2)}) collective-permute-start(f32[18,128]{1,0:T(8,128)S(1)} %get-tuple-element.25), channel_id=1, source_target_pairs={{0,2},{1,3},{2,4},{3,5},{4,6},{5,7},{6,8},{7,9},{8,10},{9,11},{10,... | collective-permute-start | bytes 27656 | tf_op jit(solution)/shard_map/ppermute | solution.py:16
  137.1 4.2 %collective-permute-start.13 = (f32[18,128]{1,0:T(8,128)S(1)}, f32[18,128]{1,0:T(8,128)S(1)}, u32[]{:S(2)}, u32[]{:S(2)}) collective-permute-start(f32[18,128]{1,0:T(8,128)S(1)} %get-tuple-element.28), channel_id=1, source_target_pairs={{0,1},{1,2},{2,3},{3,4},{4,5},{5,6},{6,7},{7,8},{8,9},{9,10},{10,1... | collective-permute-start | bytes 27656 | tf_op jit(solution)/shard_map/ppermute | solution.py:16
  142.2 3.7 %scatter_fusion.1 = f32[18,1024]{0,1:T(8,128)S(1)} fusion(f32[18,1024]{0,1:T(8,128)S(1)} %copy.52, s32[512]{0:T(512)S(1)} %fusion.20, f32[512,18]{1,0:T(8,128)S(1)} %bitcast.123), kind=kCustom, calls=%fused_computation.3 | custom fusion | flops 9216 | bytes 112640 | tf_op jit(solution)/shard_map/scatter-add | solution.py:99
  146.9 22.7 %all-reduce.4 = (f32[]{:T(128)}, f32[]{:T(128)}) all-reduce(f32[]{:T(128)} %get-tuple-element.4, f32[]{:T(128)} %get-tuple-element.3), channel_id=1, replica_groups=mesh['dom_0'=4,'dom_1'=4,'dom_2'=4,'dom_3'=2] {'dom_0'}, use_global_device_ids=true, to_apply=%region_13.15 | all-reduce | flops 2 | bytes 16 | tf_op jit(solution)/shard_map/psum | solution.py:20
  169.5 6.7 %all-reduce.2 = (f32[]{:T(128)}, f32[]{:T(128)}) all-reduce(f32[]{:T(128)} %get-tuple-element.13, f32[]{:T(128)} %get-tuple-element.14), channel_id=1, replica_groups=mesh['dom_0'=4,'dom_1'=4,'dom_2'=4,'dom_3'=2] {'dom_1'}, use_global_device_ids=true, to_apply=%region_14.16 | all-reduce | flops 2 | bytes 16 | tf_op jit(solution)/shard_map/psum | solution.py:20
  176.2 11.0 %all-reduce = (f32[]{:T(128)}, f32[]{:T(128)}) all-reduce(f32[]{:T(128)} %get-tuple-element.9, f32[]{:T(128)} %get-tuple-element.10), channel_id=1, replica_groups=mesh['dom_0'=4,'dom_1'=4,'dom_2'=4,'dom_3'=2] {'dom_2'}, use_global_device_ids=true, to_apply=%region_15.17 | all-reduce | flops 2 | bytes 16 | tf_op jit(solution)/shard_map/psum | solution.py:20
  187.2 10.2 %all-reduce.6 = (f32[]{:T(128)}, f32[]{:T(128)}) all-reduce(f32[]{:T(128)} %get-tuple-element.5, f32[]{:T(128)} %get-tuple-element.6), channel_id=1, replica_groups=mesh['dom_0'=4,'dom_1'=4,'dom_2'=4,'dom_3'=2] {'dom_3'}, use_global_device_ids=true, to_apply=%region_16.18 | all-reduce | flops 2 | bytes 16 | tf_op jit(solution)/shard_map/psum | solution.py:20
  (92 shorter events, 28.8 us)
Async XLA Ops:
  4.4 14.4 %collective-permute-start = (f32[18,128]{1,0:T(8,128)S(1)}, f32[18,128]{1,0:T(8,128)S(1)}, u32[]{:S(2)}, u32[]{:S(2)}) collective-permute-start(f32[18,128]{1,0:T(8,128)S(1)} %get-tuple-element.33), channel_id=1, source_target_pairs={{2,0},{3,1},{4,2},{5,3},{6,4},{7,5},{8,6},{9,7},{10,8},{11,9},{12,... | collective-permute-start | bytes 27656 | tf_op jit(solution)/shard_map/ppermute | solution.py:16
  5.7 13.1 %collective-permute-start.3 = (f32[18,128]{1,0:T(8,128)S(1)}, f32[18,128]{1,0:T(8,128)S(1)}, u32[]{:S(2)}, u32[]{:S(2)}) collective-permute-start(f32[18,128]{1,0:T(8,128)S(1)} %get-tuple-element.34), channel_id=1, source_target_pairs={{0,2},{1,3},{2,4},{3,5},{4,6},{5,7},{6,8},{7,9},{8,10},{9,11},{10,... | collective-permute-start | bytes 27656 | tf_op jit(solution)/shard_map/ppermute | solution.py:16
  10.3 8.5 %collective-permute-start.2 = (f32[18,128]{1,0:T(8,128)S(1)}, f32[18,128]{1,0:T(8,128)S(1)}, u32[]{:S(2)}, u32[]{:S(2)}) collective-permute-start(f32[18,128]{1,0:T(8,128)S(1)} %get-tuple-element.35), channel_id=1, source_target_pairs={{0,1},{1,2},{2,3},{3,4},{4,5},{5,6},{6,7},{7,8},{8,9},{9,10},{10,1... | collective-permute-start | bytes 27656 | tf_op jit(solution)/shard_map/ppermute | solution.py:16
  14.8 5.0 %collective-permute-start.1 = (f32[18,128]{1,0:T(8,128)S(1)}, f32[18,128]{1,0:T(8,128)S(1)}, u32[]{:S(2)}, u32[]{:S(2)}) collective-permute-start(f32[18,128]{1,0:T(8,128)S(1)} %get-tuple-element.36), channel_id=1, source_target_pairs={{1,0},{2,1},{3,2},{4,3},{5,4},{6,5},{7,6},{8,7},{9,8},{10,9},{11,1... | collective-permute-start | bytes 27656 | tf_op jit(solution)/shard_map/ppermute | solution.py:16
  25.0 21.2 %copy-start = (f32[18,1024]{1,0:T(8,128)S(1)}, f32[18,1024]{1,0:T(8,128)}, u32[]{:S(2)}) copy-start(f32[18,1024]{1,0:T(8,128)} %param.10) | copy-start | bytes 221188
  35.0 12.0 %collective-permute-start.6 = (f32[18,128]{1,0:T(8,128)S(1)}, f32[18,128]{1,0:T(8,128)S(1)}, u32[]{:S(2)}, u32[]{:S(2)}) collective-permute-start(f32[18,128]{1,0:T(8,128)S(1)} %bitcast.150), channel_id=1, source_target_pairs={{1,0},{2,1},{3,2},{4,3},{5,4},{6,5},{7,6},{8,7},{9,8},{10,9},{11,1... | collective-permute-start | bytes 27656 | tf_op jit(solution)/shard_map/ppermute | solution.py:16
  36.9 10.1 %collective-permute-start.7 = (f32[18,128]{1,0:T(8,128)S(1)}, f32[18,128]{1,0:T(8,128)S(1)}, u32[]{:S(2)}, u32[]{:S(2)}) collective-permute-start(f32[18,128]{1,0:T(8,128)S(1)} %bitcast.149), channel_id=1, source_target_pairs={{2,0},{3,1},{4,2},{5,3},{6,4},{7,5},{8,6},{9,7},{10,8},{11,9},{12,... | collective-permute-start | bytes 27656 | tf_op jit(solution)/shard_map/ppermute | solution.py:16
  38.2 8.8 %collective-permute-start.5 = (f32[18,128]{1,0:T(8,128)S(1)}, f32[18,128]{1,0:T(8,128)S(1)}, u32[]{:S(2)}, u32[]{:S(2)}) collective-permute-start(f32[18,128]{1,0:T(8,128)S(1)} %bitcast.148), channel_id=1, source_target_pairs={{0,1},{1,2},{2,3},{3,4},{4,5},{5,6},{6,7},{7,8},{8,9},{9,10},{10,1... | collective-permute-start | bytes 27656 | tf_op jit(solution)/shard_map/ppermute | solution.py:16
  42.5 4.5 %collective-permute-start.4 = (f32[18,128]{1,0:T(8,128)S(1)}, f32[18,128]{1,0:T(8,128)S(1)}, u32[]{:S(2)}, u32[]{:S(2)}) collective-permute-start(f32[18,128]{1,0:T(8,128)S(1)} %bitcast.147), channel_id=1, source_target_pairs={{0,2},{1,3},{2,4},{3,5},{4,6},{5,7},{6,8},{7,9},{8,10},{9,11},{10,... | collective-permute-start | bytes 27656 | tf_op jit(solution)/shard_map/ppermute | solution.py:16
  102.2 11.4 %collective-permute-start.8 = (f32[18,128]{1,0:T(8,128)S(1)}, f32[18,128]{1,0:T(8,128)S(1)}, u32[]{:S(2)}, u32[]{:S(2)}) collective-permute-start(f32[18,128]{1,0:T(8,128)S(1)} %get-tuple-element.29), channel_id=1, source_target_pairs={{2,0},{3,1},{4,2},{5,3},{6,4},{7,5},{8,6},{9,7},{10,8},{11,9},{12,... | collective-permute-start | bytes 27656 | tf_op jit(solution)/shard_map/ppermute | solution.py:16
  103.5 10.1 %collective-permute-start.10 = (f32[18,128]{1,0:T(8,128)S(1)}, f32[18,128]{1,0:T(8,128)S(1)}, u32[]{:S(2)}, u32[]{:S(2)}) collective-permute-start(f32[18,128]{1,0:T(8,128)S(1)} %get-tuple-element.31), channel_id=1, source_target_pairs={{0,1},{1,2},{2,3},{3,4},{4,5},{5,6},{6,7},{7,8},{8,9},{9,10},{10,1... | collective-permute-start | bytes 27656 | tf_op jit(solution)/shard_map/ppermute | solution.py:16
  108.0 5.6 %collective-permute-start.9 = (f32[18,128]{1,0:T(8,128)S(1)}, f32[18,128]{1,0:T(8,128)S(1)}, u32[]{:S(2)}, u32[]{:S(2)}) collective-permute-start(f32[18,128]{1,0:T(8,128)S(1)} %get-tuple-element.32), channel_id=1, source_target_pairs={{1,0},{2,1},{3,2},{4,3},{5,4},{6,5},{7,6},{8,7},{9,8},{10,9},{11,1... | collective-permute-start | bytes 27656 | tf_op jit(solution)/shard_map/ppermute | solution.py:16
  109.9 4.5 %collective-permute-start.11 = (f32[18,128]{1,0:T(8,128)S(1)}, f32[18,128]{1,0:T(8,128)S(1)}, u32[]{:S(2)}, u32[]{:S(2)}) collective-permute-start(f32[18,128]{1,0:T(8,128)S(1)} %get-tuple-element.30), channel_id=1, source_target_pairs={{0,2},{1,3},{2,4},{3,5},{4,6},{5,7},{6,8},{7,9},{8,10},{9,11},{10,... | collective-permute-start | bytes 27656 | tf_op jit(solution)/shard_map/ppermute | solution.py:16
  128.7 12.8 %collective-permute-start.12 = (f32[18,128]{1,0:T(8,128)S(1)}, f32[18,128]{1,0:T(8,128)S(1)}, u32[]{:S(2)}, u32[]{:S(2)}) collective-permute-start(f32[18,128]{1,0:T(8,128)S(1)} %get-tuple-element.25), channel_id=1, source_target_pairs={{0,2},{1,3},{2,4},{3,5},{4,6},{5,7},{6,8},{7,9},{8,10},{9,11},{10,... | collective-permute-start | bytes 27656 | tf_op jit(solution)/shard_map/ppermute | solution.py:16
  132.3 9.2 %collective-permute-start.15 = (f32[18,128]{1,0:T(8,128)S(1)}, f32[18,128]{1,0:T(8,128)S(1)}, u32[]{:S(2)}, u32[]{:S(2)}) collective-permute-start(f32[18,128]{1,0:T(8,128)S(1)} %get-tuple-element.26), channel_id=1, source_target_pairs={{2,0},{3,1},{4,2},{5,3},{6,4},{7,5},{8,6},{9,7},{10,8},{11,9},{12,... | collective-permute-start | bytes 27656 | tf_op jit(solution)/shard_map/ppermute | solution.py:16
  133.6 7.9 %collective-permute-start.14 = (f32[18,128]{1,0:T(8,128)S(1)}, f32[18,128]{1,0:T(8,128)S(1)}, u32[]{:S(2)}, u32[]{:S(2)}) collective-permute-start(f32[18,128]{1,0:T(8,128)S(1)} %get-tuple-element.27), channel_id=1, source_target_pairs={{1,0},{2,1},{3,2},{4,3},{5,4},{6,5},{7,6},{8,7},{9,8},{10,9},{11,1... | collective-permute-start | bytes 27656 | tf_op jit(solution)/shard_map/ppermute | solution.py:16
  137.1 5.0 %collective-permute-start.13 = (f32[18,128]{1,0:T(8,128)S(1)}, f32[18,128]{1,0:T(8,128)S(1)}, u32[]{:S(2)}, u32[]{:S(2)}) collective-permute-start(f32[18,128]{1,0:T(8,128)S(1)} %get-tuple-element.28), channel_id=1, source_target_pairs={{0,1},{1,2},{2,3},{3,4},{4,5},{5,6},{6,7},{7,8},{8,9},{9,10},{10,1... | collective-permute-start | bytes 27656 | tf_op jit(solution)/shard_map/ppermute | solution.py:16
where the time goes:
time: 204 us; the launch traced here: 203 us
  blocking collectives  98.1 us (48%)
  starting transfers between devices  47.3 us (23%)
  other arithmetic  21.3 us (10%)
  matrix products  20.2 us (10%)
  between operations  7.17 us (4%)
  local copies, waits for them, and re-layouts  6.39 us (3%)
  waiting for transfers between devices  2.25 us (1%)
    psum x8, blocking collectives, by_axis(): return functools.reduce(lax.psum, axes, value)  98.1 us
    ppermute x16, starting transfers between devices, passed_along(): lax.ppermute(value, axis, [(source, source + steps) for source in range(f...  47.3 us
    dot_general x2, matrix products, operate(): lax.dot_general(spread, selector, (((1,), (1,)), ((), ())), precision=lax...  11.2 us
    dot_general x2, matrix products, operate(): jnp.dot(extended, selector, precision=lax.Precision.HIGHEST, preferred_el...  8.99 us
    reduce_sum x2, other arithmetic, operate(): jnp.sum(element_matrix.astype(jnp.float32) * picked[None, :, :], axis=1)  8.08 us
    scatter-add x2, other arithmetic, operate(): summed[:, :own_faces].at[:, send_rows].add(returned.transpose(1, 0, 2))  7.41 us
  transfers between devices with their start and end apart: 16, of which 3 were waited for; matrix products, arithmetic and copies ran while one was open for 2% of the time, Pallas kernels for 0%

commit v1 on v0

v1 whole, which is shorter than its diff:
```python
import functools

import jax
import jax.numpy as jnp
from jax import lax
from jax.experimental import pallas as pl
from jax.experimental.pallas import tpu as pltpu
from jax.sharding import PartitionSpec as P

TRACE = 18
ROWS = 24
SIDES = 4
DOFS = 72
E_DEV = 512
F_DEV = 1024
GH = 128
OFFSETS = (-2, -1, 1, 2)
N_DOM = 128
LANES = 128
WIDE = 256
MESH = pl.DeviceIdType.MESH


def lane_pick(blocks, index_row):
    low = jnp.broadcast_to(index_row & (LANES - 1), (ROWS, LANES))
    high = jnp.broadcast_to(index_row >> 7, (ROWS, LANES))
    picked = jnp.zeros((ROWS, LANES), jnp.float32)
    for at, block in enumerate(blocks):
        moved = jnp.take_along_axis(block, low, axis=1, mode="promise_in_bounds")
        picked = jnp.where(high == at, moved, picked)
    return picked


def split_two(value):
    head = value.astype(jnp.bfloat16)
    tail = (value - head.astype(jnp.float32)).astype(jnp.bfloat16)
    return head.astype(jnp.float32), tail.astype(jnp.float32)


def spread_rows(value, index_row, groups):
    head, tail = split_two(value)
    high = jnp.broadcast_to(index_row >> 8, value.shape)
    pieces = []
    for group in range(groups):
        mask = high == group
        pieces.append(jnp.where(mask, head, 0.0))
        pieces.append(jnp.where(mask, tail, 0.0))
    return jnp.concatenate(pieces, axis=0).astype(jnp.bfloat16)


def one_hot_low(index_row):
    count = index_row.shape[1]
    low = jnp.broadcast_to(index_row & (WIDE - 1), (WIDE, count))
    rows = lax.broadcasted_iota(jnp.int32, (WIDE, count), 0)
    return jnp.where(rows == low, 1.0, 0.0).astype(jnp.bfloat16)


def nt_dot(left, right):
    return lax.dot_general(left, right, (((1,), (1,)), ((), ())), preferred_element_type=jnp.float32)


def kernel(
    right_hbm, matrix_hbm, map_hbm, share_hbm, count_hbm, mass_hbm, absorb_hbm, imped_hbm,
    x_hbm, r_hbm,
    right_ref, map_ref, share_ref, count_ref, mass_ref, absorb_ref, imped_ref, x_ref, r_ref, load_sem, store_sem,
    matrix, field0, field1, image, diag, picked0, picked1, product, hot, hot_share,
    out_buf, ghost_buf, part_buf, back_buf, sum_buf, sum_in,
    matrix_sem, out_send, out_recv, part_send, part_recv, sum_send, sum_recv,
):
    me = lax.axis_index("dom")
    loads = [
        pltpu.make_async_copy(source, target, load_sem.at[at])
        for at, (source, target) in enumerate((
            (share_hbm, share_ref), (count_hbm, count_ref), (right_hbm, right_ref), (map_hbm, map_ref),
            (mass_hbm, mass_ref), (absorb_hbm, absorb_ref), (imped_hbm, imped_ref),
        ))
    ]
    for load in loads:
        load.start()
    matrix_copy = pltpu.make_async_copy(matrix_hbm, matrix, matrix_sem)
    matrix_copy.start()

    core = lax.rem(me, 2)
    at_x = lax.rem(me // 2, 4)
    at_y = lax.rem(me // 8, 4)
    at_z = me // 32

    def line_partner(axis, step):
        if axis == 0:
            return me + 1 - 2 * core
        place, stride = ((at_x, 2), (at_y, 8), (at_z, 32))[axis - 1]
        return me + (lax.rem(place + step, 4) - place) * stride

    inside_to = [(me + o >= 0) & (me + o < N_DOM) for o in OFFSETS]
    inside_from = [(me - o >= 0) & (me - o < N_DOM) for o in OFFSETS]

    barrier = pltpu.get_barrier_semaphore()
    arrivals = jnp.int32(10)
    for k, o in enumerate(OFFSETS):
        @pl.when(inside_to[k])
        def _():
            pl.semaphore_signal(barrier, inc=1, device_id=(me + o,), device_id_type=MESH)
        arrivals = arrivals + inside_from[k].astype(jnp.int32)
    for axis in range(4):
        for step in range(1, 2 if axis == 0 else 4):
            pl.semaphore_signal(
                barrier, inc=1, device_id=(line_partner(axis, step),), device_id_type=MESH
            )

    for load in loads:
        load.wait()
    field0[0:TRACE, :] = right_ref[...]
    field0[TRACE:ROWS, :] = jnp.zeros((ROWS - TRACE, F_DEV), jnp.float32)
    diag[...] = mass_ref[...] + absorb_ref[...].astype(jnp.float32) * imped_ref[...]
    for k in range(4):
        @pl.when(jnp.logical_not(inside_from[k]))
        def _():
            for turn in range(2):
                ghost_buf[turn, k] = jnp.zeros((ROWS, GH), jnp.float32)
        @pl.when(jnp.logical_not(inside_to[k]))
        def _():
            for turn in range(2):
                back_buf[turn, k] = jnp.zeros((ROWS, GH), jnp.float32)

    lane = lax.broadcasted_iota(jnp.int32, (ROWS, GH), 1)
    alive = [lane < count_ref[0, k] for k in range(4)]

    def own_blocks(ref):
        return [ref[:, b * LANES:(b + 1) * LANES] for b in range(F_DEV // LANES)]

    def out_copy(turn, k):
        return pltpu.make_async_remote_copy(
            src_ref=out_buf.at[turn, k], dst_ref=ghost_buf.at[turn, k],
            send_sem=out_send.at[turn, k], recv_sem=out_recv.at[turn, k],
            device_id=(me + OFFSETS[k],), device_id_type=MESH,
        )

    def part_copy(turn, k):
        return pltpu.make_async_remote_copy(
            src_ref=part_buf.at[turn, k], dst_ref=back_buf.at[turn, k],
            send_sem=part_send.at[turn, k], recv_sem=part_recv.at[turn, k],
            device_id=(me - OFFSETS[k],), device_id_type=MESH,
        )

    def send_out(turn, ref):
        blocks = own_blocks(ref)
        for k in range(4):
            gone = lane_pick(blocks, share_ref[k:k + 1, :])
            out_buf[turn, k] = jnp.where(alive[k], gone, 0.0)
        if turn == 0:
            pl.semaphore_wait(barrier, arrivals)
        for k in range(4):
            @pl.when(inside_to[k])
            def _():
                out_copy(turn, k).start()

    def await_out(turn):
        for k in range(4):
            @pl.when(inside_from[k])
            def _():
                out_copy(turn, k).wait_recv()

    def send_part(turn):
        for k in range(4):
            @pl.when(inside_from[k])
            def _():
                part_copy(turn, k).start()

    def await_part(turn):
        for k in range(4):
            @pl.when(inside_to[k])
            def _():
                part_copy(turn, k).wait_recv()

    def pick_all(turn, ref, store):
        blocks = own_blocks(ref) + [ghost_buf[turn, k] for k in range(4)]
        for side in range(SIDES):
            for b in range(E_DEV // LANES):
                cols = slice(b * LANES, (b + 1) * LANES)
                store(side, b, lane_pick(blocks, map_ref[side:side + 1, cols]))

    def multiply(picked):
        for b in range(E_DEV // LANES):
            cols = slice(b * LANES, (b + 1) * LANES)
            total = jnp.zeros((DOFS, LANES), jnp.float32)
            for side in range(SIDES):
                def one(c, total):
                    row = picked[side, b, pl.ds(c, 8, stride=0), :]
                    part = matrix[side * TRACE + c, :, cols].astype(jnp.float32)
                    return total + (part.reshape(DOFS // 8, 8, LANES) * row[None]).reshape(DOFS, LANES)
                total = lax.fori_loop(0, TRACE, one, total, unroll=6)
            for side in range(SIDES):
                product[side, 0:TRACE, cols] = total[side * TRACE:(side + 1) * TRACE]

    def energy(picked):
        total = jnp.zeros((8, LANES), jnp.float32)
        for side in range(SIDES):
            for b in range(E_DEV // LANES):
                cols = slice(b * LANES, (b + 1) * LANES)
                both = picked[side, b] * product[side, :, cols]
                total = total + both[0:8] + both[8:16] + both[16:24]
        return total

    def face_sums(ref):
        square = jnp.zeros((8, LANES), jnp.float32)
        weighted = jnp.zeros((8, LANES), jnp.float32)
        for b in range(F_DEV // LANES):
            value = ref[:, b * LANES:(b + 1) * LANES]
            both = value * value
            both = both[0:8] + both[8:16] + both[16:24]
            square = square + both
            weighted = weighted + both * diag[b:b + 1, :]
        return square, weighted

    def scatter(turn, ref):
        total = jnp.zeros((6 * 2 * ROWS, WIDE), jnp.float32)
        for side in range(SIDES):
            left = spread_rows(product[side], map_ref[side:side + 1, :], 6)
            total = total + nt_dot(left, hot[:, side * E_DEV:(side + 1) * E_DEV])
        for group in range(6):
            base = group * 2 * ROWS
            both = total[base:base + ROWS] + total[base + ROWS:base + 2 * ROWS]
            if group >= 4:
                part_buf[turn, 2 * (group - 4)] = both[:, 0:GH]
                part_buf[turn, 2 * (group - 4) + 1] = both[:, GH:]
            else:
                for half in range(2):
                    b = 2 * group + half
                    cols = slice(b * LANES, (b + 1) * LANES)
                    image[turn, :, cols] = (
                        both[:, half * LANES:(half + 1) * LANES] + diag[b:b + 1, :] * ref[:, cols]
                    )

    def add_back(turn):
        total = jnp.zeros((4 * 2 * ROWS, WIDE), jnp.float32)
        for k in range(4):
            value = jnp.where(alive[k], back_buf[turn, k], 0.0)
            left = spread_rows(value, share_ref[k:k + 1, :], 4)
            total = total + nt_dot(left, hot_share[:, k * GH:(k + 1) * GH])
        for group in range(4):
            base = group * 2 * ROWS
            both = total[base:base + ROWS] + total[base + ROWS:base + 2 * ROWS]
            cols = slice(group * WIDE, (group + 1) * WIDE)
            image[turn, :, cols] = image[turn, :, cols] + both

    def sum_copy(turn, axis, step):
        return pltpu.make_async_remote_copy(
            src_ref=sum_buf.at[turn, axis], dst_ref=sum_in.at[turn, axis, step - 1],
            send_sem=sum_send.at[turn, axis, step - 1], recv_sem=sum_recv.at[turn, axis, step - 1],
            device_id=(line_partner(axis, step),), device_id_type=MESH,
        )

    def axis_steps(axis):
        return range(1, 2 if axis == 0 else 4)

    def sum_start(turn, axis, tile):
        sum_buf[turn, axis] = tile
        for step in axis_steps(axis):
            sum_copy(turn, axis, step).start()

    def sum_finish(turn, axis):
        tile = sum_buf[turn, axis]
        for step in axis_steps(axis):
            sum_copy(turn, axis, step).wait_recv()
        for step in axis_steps(axis):
            tile = tile + sum_in[turn, axis, step - 1]
        return tile

    def pack(first, second):
        row = lax.broadcasted_iota(jnp.int32, (8, LANES), 0)
        return jnp.where(
            row == 0,
            jnp.sum(first, axis=0, keepdims=True),
            jnp.where(row == 1, jnp.sum(second, axis=0, keepdims=True), 0.0),
        )

    def unpack(tile):
        total = jnp.sum(tile, axis=1, keepdims=True)
        return total[0:1], total[1:2]

    def clear_tail(ref):
        for side in range(SIDES):
            ref[side, TRACE:ROWS, :] = jnp.zeros((ROWS - TRACE, E_DEV), jnp.float32)

    send_out(0, field0)
    clear_tail(product)
    for side in range(SIDES):
        hot[:, side * E_DEV:(side + 1) * E_DEV] = one_hot_low(map_ref[side:side + 1, :])
    for k in range(4):
        hot_share[:, k * GH:(k + 1) * GH] = one_hot_low(share_ref[k:k + 1, :])
    square, weighted = face_sums(field0)
    matrix_copy.wait()
    await_out(0)

    def keep0(side, b, value):
        picked0[side, b] = value

    pick_all(0, field0, keep0)
    multiply(picked0)
    tile = pack(square, weighted + energy(picked0))
    sum_start(0, 3, tile)
    scatter(0, field0)
    send_part(0)
    sum_start(0, 2, sum_finish(0, 3))
    await_part(0)
    add_back(0)
    send_out(1, image.at[0])
    sum_start(0, 1, sum_finish(0, 2))
    sum_start(0, 0, sum_finish(0, 1))
    norm0, curve0 = unpack(sum_finish(0, 0))
    step0 = norm0 / curve0
    for b in range(F_DEV // LANES):
        cols = slice(b * LANES, (b + 1) * LANES)
        field1[:, cols] = field0[:, cols] - step0 * image[0, :, cols]
    square, weighted = face_sums(field1)
    await_out(1)

    def keep1(side, b, value):
        picked1[side, b] = picked0[side, b] - step0 * value

    pick_all(1, image.at[0], keep1)
    multiply(picked1)
    tile = pack(square, weighted + energy(picked1))
    sum_start(1, 3, tile)
    scatter(1, field1)
    send_part(1)
    sum_start(1, 2, sum_finish(1, 3))
    await_part(1)
    add_back(1)
    sum_start(1, 1, sum_finish(1, 2))
    sum_start(1, 0, sum_finish(1, 1))
    norm1, curve1 = unpack(sum_finish(1, 0))
    ratio = norm1 / norm0
    step1 = norm1 / (curve1 - ratio * norm1 / step0)
    for b in range(F_DEV // LANES):
        cols = slice(b * LANES, (b + 1) * LANES)
        start = field0[0:TRACE, cols]
        later = field1[0:TRACE, cols]
        x_ref[:, cols] = step0 * start + step1 * (later + ratio * start)
        r_ref[:, cols] = later - step1 * (image[1, 0:TRACE, cols] + ratio * image[0, 0:TRACE, cols])

    stores = [
        pltpu.make_async_copy(source, target, store_sem.at[at])
        for at, (source, target) in enumerate(((x_ref, x_hbm), (r_ref, r_hbm)))
    ]
    for store in stores:
        store.start()
    for store in stores:
        store.wait()
    for turn in range(2):
        for k in range(4):
            @pl.when(inside_to[k])
            def _():
                out_copy(turn, k).wait_send()
            @pl.when(inside_from[k])
            def _():
                part_copy(turn, k).wait_send()
        for axis in range(4):
            for step in axis_steps(axis):
                sum_copy(turn, axis, step).wait_send()


def shards(right_side, element_matrix, face_map, share_index, share_count, face_mass, absorbing, impedance):
    hbm = pl.BlockSpec(memory_space=pltpu.HBM)
    f32, bf16, i32 = jnp.float32, jnp.bfloat16, jnp.int32
    out = jax.ShapeDtypeStruct((TRACE, F_DEV), f32)
    return pl.pallas_call(
        kernel,
        name="trace_cg",
        out_shape=(out, out),
        in_specs=[hbm] * 8,
        out_specs=(hbm, hbm),
        scratch_shapes=[
            pltpu.VMEM((TRACE, F_DEV), f32),
            pltpu.VMEM((SIDES, E_DEV), i32),
            pltpu.VMEM((4, GH), i32),
            pltpu.SMEM((1, 4), i32),
            pltpu.VMEM((8, LANES), f32),
            pltpu.VMEM((8, LANES), i32),
            pltpu.VMEM((8, LANES), f32),
            pltpu.VMEM((TRACE, F_DEV), f32),
            pltpu.VMEM((TRACE, F_DEV), f32),
            pltpu.SemaphoreType.DMA((7,)),
            pltpu.SemaphoreType.DMA((2,)),
            pltpu.VMEM((DOFS, DOFS, E_DEV), bf16),
            pltpu.VMEM((ROWS, F_DEV), f32),
            pltpu.VMEM((ROWS, F_DEV), f32),
            pltpu.VMEM((2, ROWS, F_DEV), f32),
            pltpu.VMEM((8, LANES), f32),
            pltpu.VMEM((SIDES, 4, ROWS, LANES), f32),
            pltpu.VMEM((SIDES, 4, ROWS, LANES), f32),
            pltpu.VMEM((SIDES, ROWS, E_DEV), f32),
            pltpu.VMEM((WIDE, SIDES * E_DEV), bf16),
            pltpu.VMEM((WIDE, 4 * GH), bf16),
            pltpu.VMEM((2, 4, ROWS, GH), f32),
            pltpu.VMEM((2, 4, ROWS, GH), f32),
            pltpu.VMEM((2, 4, ROWS, GH), f32),
            pltpu.VMEM((2, 4, ROWS, GH), f32),
            pltpu.VMEM((2, 4, 8, LANES), f32),
            pltpu.VMEM((2, 4, 3, 8, LANES), f32),
            pltpu.SemaphoreType.DMA,
            pltpu.SemaphoreType.DMA((2, 4)),
            pltpu.SemaphoreType.DMA((2, 4)),
            pltpu.SemaphoreType.DMA((2, 4)),
            pltpu.SemaphoreType.DMA((2, 4)),
            pltpu.SemaphoreType.DMA((2, 4, 3)),
            pltpu.SemaphoreType.DMA((2, 4, 3)),
        ],
        compiler_params=pltpu.CompilerParams(
            collective_id=0, has_side_effects=True, vmem_limit_bytes=67043328
        ),
    )(
        right_side, element_matrix, face_map, share_index.reshape(4, GH), share_count,
        face_mass.reshape(8, LANES), absorbing.reshape(8, LANES), impedance.reshape(8, LANES),
    )


def solution(mesh):
    in_specs = (
        P(None, "dom"), P(None, None, "dom"), P(None, "dom"), P("dom", None, None),
        P("dom", None), P("dom"), P("dom"), P("dom"),
    )
    return jax.shard_map(
        shards, mesh=mesh, in_specs=in_specs,
        out_specs=(P(None, "dom"), P(None, "dom")), check_vma=False,
    )
```

time: 204 us -> 45.2 us (0.22)
  blocking collectives: 98.1 us -> 0 us
  starting transfers between devices: 47.3 us -> 0 us
  Pallas kernels: 0 us -> 41.3 us
  other arithmetic: 21.3 us -> 0 us
  matrix products: 20.2 us -> 0 us
  between operations: 7.17 us -> 0.64 us
  local copies, waits for them, and re-layouts: 6.39 us -> 3.08 us
  waiting for transfers between devices: 2.25 us -> 0 us
    psum x8 -> x0, blocking collectives: 98.1 us -> none  [by_axis(): return functools.reduce(lax.psum, axes, value)]
    ppermute x16 -> x0, starting transfers between devices: 47.3 us -> none  [passed_along(): lax.ppermute(value, axis, [(source, source + steps) for source in range(f...]
    pallas_call x0 -> x1, Pallas kernels: none -> 41.3 us  [shards(): pl.pallas_call(kernel, name='trace_cg', out_shape=(out, out), in_specs=[h...]
    dot_general x4 -> x0, matrix products: 20.2 us -> none  [the longest x2 11.2 us: operate(): lax.dot_general(spread, selector, (((1,), (1,)), ((), ())), precision=lax...]
    reduce_sum x5 -> x0, other arithmetic: 10.1 us -> none  [the longest x2 8.08 us: operate(): jnp.sum(element_matrix.astype(jnp.float32) * picked[None, :, :], axis=1)]
    scatter-add x2 -> x0, other arithmetic: 7.41 us -> none  [operate(): summed[:, :own_faces].at[:, send_rows].add(returned.transpose(1, 0, 2))]
    gather x4 -> x0, local copies, waits for them, and re-layouts: 2.3 us -> none  [operate(): jnp.take(field_now, send_rows, axis=1).transpose(1, 0, 2)]
    ppermute x16 -> x0, waiting for transfers between devices: 2.25 us -> none  [passed_along(): lax.ppermute(value, axis, [(source, source + steps) for source in range(f...]
  transfers between devices with their start and end apart: 16 -> 0, of which waited for: 3 -> 0; matrix products, arithmetic and copies ran while one was open for 2% -> 0% of each run, Pallas kernels for 0% -> 0%
where the time goes in v1:
time: 45.2 us; the launch traced here: 45 us
  Pallas kernels  41.3 us (91%)
  local copies, waits for them, and re-layouts  3.08 us (7%)
  between operations  0.64 us (1%)
    pallas_call x1, Pallas kernels, shards(): pl.pallas_call(kernel, name='trace_cg', out_shape=(out, out), in_specs=[h...  41.3 us
    unnamed x2, local copies, waits for them, and re-layouts  3.08 us

profile of v1, /device:TPU:1, one launch (start us, length us, event | category | flops | bytes accessed | tf_op | source)
XLA Modules:
  0.0 45.0 jit_solution(17772006143890105452)
XLA Ops:
  0.6 41.3 %trace_cg.1 = (f32[18,1024]{1,0:T(8,128)}, f32[18,1024]{1,0:T(8,128)}) custom-call(f32[18,1024]{1,0:T(8,128)} %right_hbm.1, bf16[72,72,512]{2,1,0:T(8,128)(2,1)} %matrix_hbm.1, s32[4,512]{1,0:T(4,128)} %map_hbm.1, s32[4,128]{1,0:T(4,128)} %bitcast.7, s32[1,4]{1,0:T(1,128)} %count_hbm.1, f32[8,128]{1,0:T(8,128)} %bitcast.4, s32[8,128]{1,0:T(8,128)} %bitcast.5, ...), custom_call_target="tpu_custom_call" | custom-call | tf_op jit(solution)/shard_map/trace_cg/pallas_call | solution.py:367
  41.9 1.5 %copy.12 = f32[18,1024]{1,0:T(8,128)} copy(f32[18,1024]{1,0:T(8,128)} %get-tuple-element.4) | data formatting | bytes 147456
  43.5 1.5 %copy.13 = f32[18,1024]{1,0:T(8,128)} copy(f32[18,1024]{1,0:T(8,128)} %get-tuple-element.5) | data formatting | bytes 147456

commit v2 on v1

--- a/solution.py
+++ b/solution.py
@@ -22,13 +22,17 @@
 
 
 def lane_pick(blocks, index_row):
-    low = jnp.broadcast_to(index_row & (LANES - 1), (ROWS, LANES))
-    high = jnp.broadcast_to(index_row >> 7, (ROWS, LANES))
-    picked = jnp.zeros((ROWS, LANES), jnp.float32)
-    for at, block in enumerate(blocks):
-        moved = jnp.take_along_axis(block, low, axis=1, mode="promise_in_bounds")
-        picked = jnp.where(high == at, moved, picked)
-    return picked
+    low = jnp.broadcast_to(index_row & (LANES - 1), (8, LANES))
+    high = jnp.broadcast_to(index_row >> 7, (8, LANES))
+    masks = [high == at for at in range(len(blocks))]
+    pieces = []
+    for i in range(ROWS // 8):
+        picked = jnp.zeros((8, LANES), jnp.float32)
+        for mask, block in zip(masks, blocks):
+            moved = jnp.take_along_axis(block(i), low, axis=1, mode="promise_in_bounds")
+            picked = jnp.where(mask, moved, picked)
+        pieces.append(picked)
+    return jnp.concatenate(pieces, axis=0)
 
 
 def split_two(value):
@@ -61,9 +65,9 @@
 
 def kernel(
     right_hbm, matrix_hbm, map_hbm, share_hbm, count_hbm, mass_hbm, absorb_hbm, imped_hbm,
-    x_hbm, r_hbm,
-    right_ref, map_ref, share_ref, count_ref, mass_ref, absorb_ref, imped_ref, x_ref, r_ref, load_sem, store_sem,
-    matrix, field0, field1, image, diag, picked0, picked1, product, hot, hot_share,
+    lead_ref, later_ref, along_ref, step_ref,
+    right_ref, map_ref, share_ref, count_ref, mass_ref, absorb_ref, imped_ref, load_sem, meet_sem,
+    matrix, widened, field0, field1, image, diag, picked0, picked1, product, hot, hot_share,
     out_buf, ghost_buf, part_buf, back_buf, sum_buf, sum_in,
     matrix_sem, out_send, out_recv, part_send, part_recv, sum_send, sum_recv,
 ):
@@ -85,27 +89,33 @@
     at_y = lax.rem(me // 8, 4)
     at_z = me // 32
 
-    def line_partner(axis, step):
-        if axis == 0:
-            return me + 1 - 2 * core
-        place, stride = ((at_x, 2), (at_y, 8), (at_z, 32))[axis - 1]
-        return me + (lax.rem(place + step, 4) - place) * stride
+    along_x = [lax.rem(at_x + d, 4) * 2 for d in range(4)]
+    along_y = [lax.rem(at_y + d, 4) * 8 for d in range(4)]
+    along_z = [lax.rem(at_z + d, 4) * 32 for d in range(4)]
+    cores = (core, 1 - core)
+
+    def device_at(dz, dy, dx, dc):
+        return along_z[dz] + along_y[dy] + along_x[dx] + cores[dc]
 
     inside_to = [(me + o >= 0) & (me + o < N_DOM) for o in OFFSETS]
     inside_from = [(me - o >= 0) & (me - o < N_DOM) for o in OFFSETS]
 
     barrier = pltpu.get_barrier_semaphore()
-    arrivals = jnp.int32(10)
+    arrivals = jnp.int32(13)
     for k, o in enumerate(OFFSETS):
         @pl.when(inside_to[k])
         def _():
             pl.semaphore_signal(barrier, inc=1, device_id=(me + o,), device_id_type=MESH)
         arrivals = arrivals + inside_from[k].astype(jnp.int32)
-    for axis in range(4):
-        for step in range(1, 2 if axis == 0 else 4):
-            pl.semaphore_signal(
-                barrier, inc=1, device_id=(line_partner(axis, step),), device_id_type=MESH
-            )
+    line_y = [device_at(0, d, 0, 0) for d in range(1, 4)]
+    line_z = [device_at(d, 0, 0, 0) for d in range(1, 4)]
+    pairs_x = [device_at(0, 0, d, c) for d in range(4) for c in range(2) if d or c]
+    for other in pairs_x + line_y + line_z:
+        pl.semaphore_signal(barrier, inc=1, device_id=(other,), device_id_type=MESH)
+
+    def meet(at, others):
+        for other in others:
+            pl.semaphore_signal(meet_sem.at[at], inc=1, device_id=(other,), device_id_type=MESH)
 
     for load in loads:
         load.wait()
@@ -126,7 +136,9 @@
     alive = [lane < count_ref[0, k] for k in range(4)]
 
     def own_blocks(ref):
-        return [ref[:, b * LANES:(b + 1) * LANES] for b in range(F_DEV // LANES)]
+        return [
+            lambda i, b=b: ref[8 * i:8 * i + 8, b * LANES:(b + 1) * LANES] for b in range(F_DEV // LANES)
+        ]
 
     def out_copy(turn, k):
         return pltpu.make_async_remote_copy(
@@ -173,7 +185,9 @@
                 part_copy(turn, k).wait_recv()
 
     def pick_all(turn, ref, store):
-        blocks = own_blocks(ref) + [ghost_buf[turn, k] for k in range(4)]
+        blocks = own_blocks(ref) + [
+            lambda i, k=k: ghost_buf[turn, k, 8 * i:8 * i + 8] for k in range(4)
+        ]
         for side in range(SIDES):
             for b in range(E_DEV // LANES):
                 cols = slice(b * LANES, (b + 1) * LANES)
@@ -186,7 +200,7 @@
             for side in range(SIDES):
                 def one(c, total):
                     row = picked[side, b, pl.ds(c, 8, stride=0), :]
-                    part = matrix[side * TRACE + c, :, cols].astype(jnp.float32)
+                    part = widened[side * TRACE + c, :, cols]
                     return total + (part.reshape(DOFS // 8, 8, LANES) * row[None]).reshape(DOFS, LANES)
                 total = lax.fori_loop(0, TRACE, one, total, unroll=6)
             for side in range(SIDES):
@@ -243,53 +257,62 @@
             cols = slice(group * WIDE, (group + 1) * WIDE)
             image[turn, :, cols] = image[turn, :, cols] + both
 
-    def sum_copy(turn, axis, step):
-        return pltpu.make_async_remote_copy(
-            src_ref=sum_buf.at[turn, axis], dst_ref=sum_in.at[turn, axis, step - 1],
-            send_sem=sum_send.at[turn, axis, step - 1], recv_sem=sum_recv.at[turn, axis, step - 1],
-            device_id=(line_partner(axis, step),), device_id_type=MESH,
+    others = sorted(
+        ((dz, dy, dx, dc) for dz in range(4) for dy in range(4) for dx in range(4) for dc in range(2) if dz or dy or dx or dc),
+        key=lambda at: -sum(min(d, 4 - d) for d in at[:3]),
+    )
+
+    def sum_start(turn, square, weighted):
+        lane_at = lax.broadcasted_iota(jnp.int32, (1, LANES), 1)
+        first = jnp.sum(square, axis=0, keepdims=True)
+        second = jnp.sum(weighted, axis=0, keepdims=True)
+        first = first + pltpu.roll(first, LANES // 2, 1)
+        second = second + pltpu.roll(second, LANES // 2, 1)
+        row = jnp.where(lane_at < LANES // 2, first, second)
+        sum_buf[turn] = row
+        sum_in[turn, me] = row
+        for at in others:
+            pltpu.make_async_remote_copy(
+                src_ref=sum_buf.at[turn], dst_ref=sum_in.at[turn, me],
+                send_sem=sum_send.at[turn], recv_sem=sum_recv.at[turn],
+                device_id=(device_at(*at),), device_id_type=MESH,
+            ).start()
+
+    def sum_whole(turn, sem):
+        return pltpu.make_async_copy(
+            sum_in.at[turn, pl.ds(0, N_DOM - 1)], sum_in.at[turn, pl.ds(1, N_DOM - 1)], sem.at[turn]
         )
 
-    def axis_steps(axis):
-        return range(1, 2 if axis == 0 else 4)
-
-    def sum_start(turn, axis, tile):
-        sum_buf[turn, axis] = tile
-        for step in axis_steps(axis):
-            sum_copy(turn, axis, step).start()
-
-    def sum_finish(turn, axis):
-        tile = sum_buf[turn, axis]
-        for step in axis_steps(axis):
-            sum_copy(turn, axis, step).wait_recv()
-        for step in axis_steps(axis):
-            tile = tile + sum_in[turn, axis, step - 1]
-        return tile
-
-    def pack(first, second):
-        row = lax.broadcasted_iota(jnp.int32, (8, LANES), 0)
-        return jnp.where(
-            row == 0,
-            jnp.sum(first, axis=0, keepdims=True),
-            jnp.where(row == 1, jnp.sum(second, axis=0, keepdims=True), 0.0),
-        )
-
-    def unpack(tile):
-        total = jnp.sum(tile, axis=1, keepdims=True)
-        return total[0:1], total[1:2]
+    def sum_finish(turn):
+        sum_whole(turn, sum_recv).wait()
+        total = jnp.sum(sum_in[turn], axis=0)
+        lane_at = lax.broadcasted_iota(jnp.int32, (1, LANES), 1)
+        first = jnp.sum(jnp.where(lane_at < LANES // 2, total, 0.0), axis=1, keepdims=True)
+        second = jnp.sum(jnp.where(lane_at < LANES // 2, 0.0, total), axis=1, keepdims=True)
+        return first, second
 
     def clear_tail(ref):
         for side in range(SIDES):
             ref[side, TRACE:ROWS, :] = jnp.zeros((ROWS - TRACE, E_DEV), jnp.float32)
 
     send_out(0, field0)
+    meet(0, line_y)
     clear_tail(product)
     for side in range(SIDES):
         hot[:, side * E_DEV:(side + 1) * E_DEV] = one_hot_low(map_ref[side:side + 1, :])
     for k in range(4):
         hot_share[:, k * GH:(k + 1) * GH] = one_hot_low(share_ref[k:k + 1, :])
     square, weighted = face_sums(field0)
+    pl.semaphore_wait(meet_sem.at[0], 3)
+    meet(1, line_z)
     matrix_copy.wait()
+
+    def widen(row, carry):
+        widened[row] = matrix[row].astype(jnp.float32)
+        return carry
+
+    lax.fori_loop(0, DOFS, widen, 0, unroll=4)
+    pl.semaphore_wait(meet_sem.at[1], 3)
     await_out(0)
 
     def keep0(side, b, value):
@@ -297,17 +320,14 @@
 
     pick_all(0, field0, keep0)
     multiply(picked0)
-    tile = pack(square, weighted + energy(picked0))
-    sum_start(0, 3, tile)
+    square0, weighted0 = square, weighted + energy(picked0)
     scatter(0, field0)
     send_part(0)
-    sum_start(0, 2, sum_finish(0, 3))
+    sum_start(0, square0, weighted0)
     await_part(0)
     add_back(0)
     send_out(1, image.at[0])
-    sum_start(0, 1, sum_finish(0, 2))
-    sum_start(0, 0, sum_finish(0, 1))
-    norm0, curve0 = unpack(sum_finish(0, 0))
+    norm0, curve0 = sum_finish(0)
     step0 = norm0 / curve0
     for b in range(F_DEV // LANES):
         cols = slice(b * LANES, (b + 1) * LANES)
@@ -320,33 +340,22 @@
 
     pick_all(1, image.at[0], keep1)
     multiply(picked1)
-    tile = pack(square, weighted + energy(picked1))
-    sum_start(1, 3, tile)
+    sum_start(1, square, weighted + energy(picked1))
     scatter(1, field1)
     send_part(1)
-    sum_start(1, 2, sum_finish(1, 3))
     await_part(1)
     add_back(1)
-    sum_start(1, 1, sum_finish(1, 2))
-    sum_start(1, 0, sum_finish(1, 1))
-    norm1, curve1 = unpack(sum_finish(1, 0))
+    norm1, curve1 = sum_finish(1)
     ratio = norm1 / norm0
     step1 = norm1 / (curve1 - ratio * norm1 / step0)
+    lead = step0 + step1 * ratio
     for b in range(F_DEV // LANES):
         cols = slice(b * LANES, (b + 1) * LANES)
-        start = field0[0:TRACE, cols]
-        later = field1[0:TRACE, cols]
-        x_ref[:, cols] = step0 * start + step1 * (later + ratio * start)
-        r_ref[:, cols] = later - step1 * (image[1, 0:TRACE, cols] + ratio * image[0, 0:TRACE, cols])
-
-    stores = [
-        pltpu.make_async_copy(source, target, store_sem.at[at])
-        for at, (source, target) in enumerate(((x_ref, x_hbm), (r_ref, r_hbm)))
-    ]
-    for store in stores:
-        store.start()
-    for store in stores:
-        store.wait()
+        lead_ref[:, cols] = lead * field0[0:TRACE, cols]
+        later_ref[:, cols] = field1[0:TRACE, cols]
+        along_ref[:, cols] = image[1, 0:TRACE, cols] + ratio * image[0, 0:TRACE, cols]
+    step_ref[...] = jnp.broadcast_to(step1, (TRACE, F_DEV))
+
     for turn in range(2):
         for k in range(4):
             @pl.when(inside_to[k])
@@ -355,21 +364,20 @@
             @pl.when(inside_from[k])
             def _():
                 part_copy(turn, k).wait_send()
-        for axis in range(4):
-            for step in axis_steps(axis):
-                sum_copy(turn, axis, step).wait_send()
+        sum_whole(turn, sum_send).wait()
 
 
 def shards(right_side, element_matrix, face_map, share_index, share_count, face_mass, absorbing, impedance):
     hbm = pl.BlockSpec(memory_space=pltpu.HBM)
     f32, bf16, i32 = jnp.float32, jnp.bfloat16, jnp.int32
-    out = jax.ShapeDtypeStruct((TRACE, F_DEV), f32)
-    return pl.pallas_call(
+    out = pltpu.VMEM((TRACE, F_DEV), f32)
+    vmem = pl.BlockSpec(memory_space=pltpu.VMEM)
+    lead, later, along, step = pl.pallas_call(
         kernel,
         name="trace_cg",
-        out_shape=(out, out),
+        out_shape=(out, out, out, out),
         in_specs=[hbm] * 8,
-        out_specs=(hbm, hbm),
+        out_specs=(vmem, vmem, vmem, vmem),
         scratch_shapes=[
             pltpu.VMEM((TRACE, F_DEV), f32),
             pltpu.VMEM((SIDES, E_DEV), i32),
@@ -378,11 +386,10 @@
             pltpu.VMEM((8, LANES), f32),
             pltpu.VMEM((8, LANES), i32),
             pltpu.VMEM((8, LANES), f32),
-            pltpu.VMEM((TRACE, F_DEV), f32),
-            pltpu.VMEM((TRACE, F_DEV), f32),
             pltpu.SemaphoreType.DMA((7,)),
-            pltpu.SemaphoreType.DMA((2,)),
+            pltpu.SemaphoreType.REGULAR((2,)),
             pltpu.VMEM((DOFS, DOFS, E_DEV), bf16),
+            pltpu.VMEM((DOFS, DOFS, E_DEV), f32),
             pltpu.VMEM((ROWS, F_DEV), f32),
             pltpu.VMEM((ROWS, F_DEV), f32),
             pltpu.VMEM((2, ROWS, F_DEV), f32),
@@ -396,23 +403,24 @@
             pltpu.VMEM((2, 4, ROWS, GH), f32),
             pltpu.VMEM((2, 4, ROWS, GH), f32),
             pltpu.VMEM((2, 4, ROWS, GH), f32),
-            pltpu.VMEM((2, 4, 8, LANES), f32),
-            pltpu.VMEM((2, 4, 3, 8, LANES), f32),
+            pltpu.VMEM((2, 1, LANES), f32),
+            pltpu.VMEM((2, N_DOM, 1, LANES), f32),
             pltpu.SemaphoreType.DMA,
             pltpu.SemaphoreType.DMA((2, 4)),
             pltpu.SemaphoreType.DMA((2, 4)),
             pltpu.SemaphoreType.DMA((2, 4)),
             pltpu.SemaphoreType.DMA((2, 4)),
-            pltpu.SemaphoreType.DMA((2, 4, 3)),
-            pltpu.SemaphoreType.DMA((2, 4, 3)),
+            pltpu.SemaphoreType.DMA((2,)),
+            pltpu.SemaphoreType.DMA((2,)),
         ],
         compiler_params=pltpu.CompilerParams(
-            collective_id=0, has_side_effects=True, vmem_limit_bytes=67043328
+            collective_id=0, has_side_effects=True, vmem_limit_bytes=65 * 1000 * 1000
         ),
     )(
         right_side, element_matrix, face_map, share_index.reshape(4, GH), share_count,
         face_mass.reshape(8, LANES), absorbing.reshape(8, LANES), impedance.reshape(8, LANES),
     )
+    return lead + step * later, later - step * along
 
 
 def solution(mesh):

time: 45.2 us -> 36.8 us (0.81)
  Pallas kernels: 41.3 us -> 35.3 us
  local copies, waits for them, and re-layouts: 3.08 us -> 0 us
  other arithmetic: 0 us -> 0.7 us
    pallas_call x1, Pallas kernels: 41.3 us -> 35.3 us  [shards(): pl.pallas_call(kernel, name='trace_cg', out_shape=(out, out, out, out), i...]
    unnamed x2 -> x0, local copies, waits for them, and re-layouts: 3.08 us -> none
    sub x0 -> x1, other arithmetic: none -> 0.7 us  [shards(): return (lead + step * later, later - step * along)]
where the time goes in v2:
time: 36.8 us; the launch traced here: 36.7 us
  Pallas kernels  35.3 us (96%)
  other arithmetic  0.7 us (2%)
  between operations  0.64 us (2%)
    pallas_call x1, Pallas kernels, shards(): pl.pallas_call(kernel, name='trace_cg', out_shape=(out, out, out, out), i...  35.3 us

profile of v2, /device:TPU:1, one launch (start us, length us, event | category | flops | bytes accessed | tf_op | source)
XLA Modules:
  0.0 36.7 jit_solution(1070225690563512454)
XLA Ops:
  0.6 35.3 %trace_cg.1 = (f32[18,1024]{1,0:T(8,128)S(1)}, f32[18,1024]{1,0:T(8,128)S(1)}, f32[18,1024]{1,0:T(8,128)S(1)}, f32[18,1024]{1,0:T(8,128)S(1)}) custom-call(f32[18,1024]{1,0:T(8,128)} %right_hbm.1, bf16[72,72,512]{2,1,0:T(8,128)(2,1)} %matrix_hbm.1, s32[4,512]{1,0:T(4,128)} %map_hbm.1, s32[4,128]{1,0:T(4,128)} %bitcast.7, s32[1,4]{1,0:T(1,128)} %count_hbm.1, ...), custom_call_target="tpu_custom_call" | custom-call | tf_op jit(solution)/shard_map/trace_cg/pallas_call | solution.py:375
  36.0 0.7 %multiply_subtract_fusion = (f32[18,1024]{1,0:T(8,128)}, f32[18,1024]{1,0:T(8,128)}) fusion(f32[18,1024]{1,0:T(8,128)S(1)} %get-tuple-element.8, f32[18,1024]{1,0:T(8,128)S(1)} %get-tuple-element.7, f32[18,1024]{1,0:T(8,128)S(1)} %get-tuple-element.9, f32[18,1024]{1,0:T(8,128)S(1)} %get-tuple-element.6), kind=kLoop, calls=%fused_computation | loop fusion | flops 73728 | bytes 442368 | tf_op jit(solution)/shard_map/sub | solution.py:423

commit v3 on v2

--- a/solution.py
+++ b/solution.py
@@ -21,13 +21,13 @@
 MESH = pl.DeviceIdType.MESH
 
 
-def lane_pick(blocks, index_row):
+def lane_pick(blocks, index_row, first, base):
     low = jnp.broadcast_to(index_row & (LANES - 1), (8, LANES))
     high = jnp.broadcast_to(index_row >> 7, (8, LANES))
-    masks = [high == at for at in range(len(blocks))]
+    masks = [high == first + at for at in range(len(blocks))]
     pieces = []
     for i in range(ROWS // 8):
-        picked = jnp.zeros((8, LANES), jnp.float32)
+        picked = jnp.zeros((8, LANES), jnp.float32) if base is None else base(i)
         for mask, block in zip(masks, blocks):
             moved = jnp.take_along_axis(block(i), low, axis=1, mode="promise_in_bounds")
             picked = jnp.where(mask, moved, picked)
@@ -45,7 +45,7 @@
     head, tail = split_two(value)
     high = jnp.broadcast_to(index_row >> 8, value.shape)
     pieces = []
-    for group in range(groups):
+    for group in groups:
         mask = high == group
         pieces.append(jnp.where(mask, head, 0.0))
         pieces.append(jnp.where(mask, tail, 0.0))
@@ -53,14 +53,15 @@
 
 
 def one_hot_low(index_row):
-    count = index_row.shape[1]
-    low = jnp.broadcast_to(index_row & (WIDE - 1), (WIDE, count))
-    rows = lax.broadcasted_iota(jnp.int32, (WIDE, count), 0)
-    return jnp.where(rows == low, 1.0, 0.0).astype(jnp.bfloat16)
-
-
-def nt_dot(left, right):
-    return lax.dot_general(left, right, (((1,), (1,)), ((), ())), preferred_element_type=jnp.float32)
+    low = (index_row & (WIDE - 1)).astype(jnp.float32)
+    column = jnp.broadcast_to(low, (LANES, LANES)).T
+    lane = lax.broadcasted_iota(jnp.int32, (LANES, LANES), 1).astype(jnp.float32)
+    halves = [jnp.where(column == lane + half * LANES, 1.0, 0.0) for half in range(2)]
+    return jnp.concatenate(halves, axis=1).astype(jnp.bfloat16)
+
+
+def wide_dot(left, right):
+    return jnp.dot(left, right, preferred_element_type=jnp.float32)
 
 
 def kernel(
@@ -157,7 +158,7 @@
     def send_out(turn, ref):
         blocks = own_blocks(ref)
         for k in range(4):
-            gone = lane_pick(blocks, share_ref[k:k + 1, :])
+            gone = lane_pick(blocks, share_ref[k:k + 1, :], 0, None)
             out_buf[turn, k] = jnp.where(alive[k], gone, 0.0)
         if turn == 0:
             pl.semaphore_wait(barrier, arrivals)
@@ -184,36 +185,39 @@
             def _():
                 part_copy(turn, k).wait_recv()
 
-    def pick_all(turn, ref, store):
-        blocks = own_blocks(ref) + [
-            lambda i, k=k: ghost_buf[turn, k, 8 * i:8 * i + 8] for k in range(4)
-        ]
+    def pick_own(ref, picked):
+        blocks = own_blocks(ref)
         for side in range(SIDES):
             for b in range(E_DEV // LANES):
                 cols = slice(b * LANES, (b + 1) * LANES)
-                store(side, b, lane_pick(blocks, map_ref[side:side + 1, cols]))
-
-    def multiply(picked):
-        for b in range(E_DEV // LANES):
-            cols = slice(b * LANES, (b + 1) * LANES)
-            total = jnp.zeros((DOFS, LANES), jnp.float32)
-            for side in range(SIDES):
-                def one(c, total):
-                    row = picked[side, b, pl.ds(c, 8, stride=0), :]
-                    part = widened[side * TRACE + c, :, cols]
-                    return total + (part.reshape(DOFS // 8, 8, LANES) * row[None]).reshape(DOFS, LANES)
-                total = lax.fori_loop(0, TRACE, one, total, unroll=6)
-            for side in range(SIDES):
-                product[side, 0:TRACE, cols] = total[side * TRACE:(side + 1) * TRACE]
-
-    def energy(picked):
-        total = jnp.zeros((8, LANES), jnp.float32)
+                picked[side, b] = lane_pick(blocks, map_ref[side:side + 1, cols], 0, None)
+
+    def pick_ghost(turn, picked, finish):
+        blocks = [lambda i, k=k: ghost_buf[turn, k, 8 * i:8 * i + 8] for k in range(4)]
         for side in range(SIDES):
             for b in range(E_DEV // LANES):
                 cols = slice(b * LANES, (b + 1) * LANES)
-                both = picked[side, b] * product[side, :, cols]
-                total = total + both[0:8] + both[8:16] + both[16:24]
-        return total
+                base = lambda i, side=side, b=b: picked[side, b, 8 * i:8 * i + 8]
+                value = lane_pick(blocks, map_ref[side:side + 1, cols], F_DEV // LANES, base)
+                picked[side, b] = finish(side, b, value)
+
+    def multiply(picked):
+        energy = jnp.zeros((TRACE, LANES), jnp.float32)
+        for b in range(E_DEV // LANES):
+            cols = slice(b * LANES, (b + 1) * LANES)
+
+            def one(side, total, b=b):
+                for c in range(TRACE):
+                    row = picked[side, b, c:c + 1, :]
+                    total = total + widened[b, side * TRACE + c] * row
+                return total
+
+            total = lax.fori_loop(0, SIDES, one, jnp.zeros((DOFS, LANES), jnp.float32))
+            for side in range(SIDES):
+                piece = total[side * TRACE:(side + 1) * TRACE]
+                product[side, 0:TRACE, cols] = piece
+                energy = energy + piece * picked[side, b, 0:TRACE, :]
+        return jnp.sum(energy, axis=0, keepdims=True)
 
     def face_sums(ref):
         square = jnp.zeros((8, LANES), jnp.float32)
@@ -224,33 +228,35 @@
             both = both[0:8] + both[8:16] + both[16:24]
             square = square + both
             weighted = weighted + both * diag[b:b + 1, :]
-        return square, weighted
-
-    def scatter(turn, ref):
-        total = jnp.zeros((6 * 2 * ROWS, WIDE), jnp.float32)
+        return jnp.sum(square, axis=0, keepdims=True), jnp.sum(weighted, axis=0, keepdims=True)
+
+    def scatter(groups):
+        total = jnp.zeros((len(groups) * 2 * ROWS, WIDE), jnp.float32)
         for side in range(SIDES):
-            left = spread_rows(product[side], map_ref[side:side + 1, :], 6)
-            total = total + nt_dot(left, hot[:, side * E_DEV:(side + 1) * E_DEV])
-        for group in range(6):
-            base = group * 2 * ROWS
-            both = total[base:base + ROWS] + total[base + ROWS:base + 2 * ROWS]
-            if group >= 4:
-                part_buf[turn, 2 * (group - 4)] = both[:, 0:GH]
-                part_buf[turn, 2 * (group - 4) + 1] = both[:, GH:]
-            else:
-                for half in range(2):
-                    b = 2 * group + half
-                    cols = slice(b * LANES, (b + 1) * LANES)
-                    image[turn, :, cols] = (
-                        both[:, half * LANES:(half + 1) * LANES] + diag[b:b + 1, :] * ref[:, cols]
-                    )
+            left = spread_rows(product[side], map_ref[side:side + 1, :], groups)
+            total = total + wide_dot(left, hot[side * E_DEV:(side + 1) * E_DEV, :])
+        for at in range(len(groups)):
+            base = at * 2 * ROWS
+            yield total[base:base + ROWS] + total[base + ROWS:base + 2 * ROWS]
+
+    def scatter_ghost(turn):
+        for at, both in enumerate(scatter((4, 5))):
+            part_buf[turn, 2 * at] = both[:, 0:GH]
+            part_buf[turn, 2 * at + 1] = both[:, GH:]
+
+    def scatter_own(turn, ref):
+        for at, both in enumerate(scatter((0, 1, 2, 3))):
+            for half in range(2):
+                b = 2 * at + half
+                cols = slice(b * LANES, (b + 1) * LANES)
+                image[turn, :, cols] = both[:, half * LANES:(half + 1) * LANES] + diag[b:b + 1, :] * ref[:, cols]
 
     def add_back(turn):
         total = jnp.zeros((4 * 2 * ROWS, WIDE), jnp.float32)
         for k in range(4):
             value = jnp.where(alive[k], back_buf[turn, k], 0.0)
-            left = spread_rows(value, share_ref[k:k + 1, :], 4)
-            total = total + nt_dot(left, hot_share[:, k * GH:(k + 1) * GH])
+            left = spread_rows(value, share_ref[k:k + 1, :], (0, 1, 2, 3))
+            total = total + wide_dot(left, hot_share[k * GH:(k + 1) * GH, :])
         for group in range(4):
             base = group * 2 * ROWS
             both = total[base:base + ROWS] + total[base + ROWS:base + 2 * ROWS]
@@ -262,10 +268,8 @@
         key=lambda at: -sum(min(d, 4 - d) for d in at[:3]),
     )
 
-    def sum_start(turn, square, weighted):
+    def sum_start(turn, first, second):
         lane_at = lax.broadcasted_iota(jnp.int32, (1, LANES), 1)
-        first = jnp.sum(square, axis=0, keepdims=True)
-        second = jnp.sum(weighted, axis=0, keepdims=True)
         first = first + pltpu.roll(first, LANES // 2, 1)
         second = second + pltpu.roll(second, LANES // 2, 1)
         row = jnp.where(lane_at < LANES // 2, first, second)
@@ -299,34 +303,37 @@
     meet(0, line_y)
     clear_tail(product)
     for side in range(SIDES):
-        hot[:, side * E_DEV:(side + 1) * E_DEV] = one_hot_low(map_ref[side:side + 1, :])
+        for b in range(E_DEV // LANES):
+            first = side * E_DEV + b * LANES
+            hot[first:first + LANES, :] = one_hot_low(map_ref[side:side + 1, b * LANES:(b + 1) * LANES])
     for k in range(4):
-        hot_share[:, k * GH:(k + 1) * GH] = one_hot_low(share_ref[k:k + 1, :])
+        hot_share[k * GH:(k + 1) * GH, :] = one_hot_low(share_ref[k:k + 1, :])
     square, weighted = face_sums(field0)
     pl.semaphore_wait(meet_sem.at[0], 3)
     meet(1, line_z)
     matrix_copy.wait()
 
     def widen(row, carry):
-        widened[row] = matrix[row].astype(jnp.float32)
+        whole = matrix[row].astype(jnp.float32)
+        for b in range(E_DEV // LANES):
+            widened[b, row] = whole[:, b * LANES:(b + 1) * LANES]
         return carry
 
-    lax.fori_loop(0, DOFS, widen, 0, unroll=4)
+    pick_own(field0, picked0)
+    lax.fori_loop(0, DOFS, widen, 0, unroll=2)
     pl.semaphore_wait(meet_sem.at[1], 3)
     await_out(0)
 
-    def keep0(side, b, value):
-        picked0[side, b] = value
-
-    pick_all(0, field0, keep0)
-    multiply(picked0)
-    square0, weighted0 = square, weighted + energy(picked0)
-    scatter(0, field0)
+    pick_ghost(0, picked0, lambda side, b, value: value)
+    weighted = weighted + multiply(picked0)
+    scatter_ghost(0)
     send_part(0)
-    sum_start(0, square0, weighted0)
+    sum_start(0, square, weighted)
+    scatter_own(0, field0)
     await_part(0)
     add_back(0)
     send_out(1, image.at[0])
+    pick_own(image.at[0], picked1)
     norm0, curve0 = sum_finish(0)
     step0 = norm0 / curve0
     for b in range(F_DEV // LANES):
@@ -334,15 +341,11 @@
         field1[:, cols] = field0[:, cols] - step0 * image[0, :, cols]
     square, weighted = face_sums(field1)
     await_out(1)
-
-    def keep1(side, b, value):
-        picked1[side, b] = picked0[side, b] - step0 * value
-
-    pick_all(1, image.at[0], keep1)
-    multiply(picked1)
-    sum_start(1, square, weighted + energy(picked1))
-    scatter(1, field1)
+    pick_ghost(1, picked1, lambda side, b, value: picked0[side, b] - step0 * value)
+    sum_start(1, square, weighted + multiply(picked1))
+    scatter_ghost(1)
     send_part(1)
+    scatter_own(1, field1)
     await_part(1)
     add_back(1)
     norm1, curve1 = sum_finish(1)
@@ -389,7 +392,7 @@
             pltpu.SemaphoreType.DMA((7,)),
             pltpu.SemaphoreType.REGULAR((2,)),
             pltpu.VMEM((DOFS, DOFS, E_DEV), bf16),
-            pltpu.VMEM((DOFS, DOFS, E_DEV), f32),
+            pltpu.VMEM((E_DEV // LANES, DOFS, DOFS, LANES), f32),
             pltpu.VMEM((ROWS, F_DEV), f32),
             pltpu.VMEM((ROWS, F_DEV), f32),
             pltpu.VMEM((2, ROWS, F_DEV), f32),
@@ -397,8 +400,8 @@
             pltpu.VMEM((SIDES, 4, ROWS, LANES), f32),
             pltpu.VMEM((SIDES, 4, ROWS, LANES), f32),
             pltpu.VMEM((SIDES, ROWS, E_DEV), f32),
-            pltpu.VMEM((WIDE, SIDES * E_DEV), bf16),
-            pltpu.VMEM((WIDE, 4 * GH), bf16),
+            pltpu.VMEM((SIDES * E_DEV, WIDE), bf16),
+            pltpu.VMEM((4 * GH, WIDE), bf16),
             pltpu.VMEM((2, 4, ROWS, GH), f32),
             pltpu.VMEM((2, 4, ROWS, GH), f32),
             pltpu.VMEM((2, 4, ROWS, GH), f32),

time: 36.8 us -> 34 us (0.924)
  Pallas kernels: 35.3 us -> 32.6 us
    pallas_call x1, Pallas kernels: 35.3 us -> 32.6 us  [shards(): pl.pallas_call(kernel, name='trace_cg', out_shape=(out, out, out, out), i...]
where the time goes in v3:
time: 34 us; the launch traced here: 33.9 us
  Pallas kernels  32.6 us (96%)
  other arithmetic  0.7 us (2%)
  between operations  0.64 us (2%)
    pallas_call x1, Pallas kernels, shards(): pl.pallas_call(kernel, name='trace_cg', out_shape=(out, out, out, out), i...  32.6 us
    sub x1, other arithmetic, shards(): return (lead + step * later, later - step * along)  0.7 us

profile of v3, /device:TPU:1, one launch (start us, length us, event | category | flops | bytes accessed | tf_op | source)
XLA Modules:
  0.0 33.9 jit_solution(10200140118527564207)
XLA Ops:
  0.6 32.6 %trace_cg.1 = (f32[18,1024]{1,0:T(8,128)S(1)}, f32[18,1024]{1,0:T(8,128)S(1)}, f32[18,1024]{1,0:T(8,128)S(1)}, f32[18,1024]{1,0:T(8,128)S(1)}) custom-call(f32[18,1024]{1,0:T(8,128)} %right_hbm.1, bf16[72,72,512]{2,1,0:T(8,128)(2,1)} %matrix_hbm.1, s32[4,512]{1,0:T(4,128)} %map_hbm.1, s32[4,128]{1,0:T(4,128)} %bitcast.7, s32[1,4]{1,0:T(1,128)} %count_hbm.1, ...), custom_call_target="tpu_custom_call" | custom-call | tf_op jit(solution)/shard_map/trace_cg/pallas_call | solution.py:378
  33.2 0.7 %multiply_subtract_fusion = (f32[18,1024]{1,0:T(8,128)}, f32[18,1024]{1,0:T(8,128)}) fusion(f32[18,1024]{1,0:T(8,128)S(1)} %get-tuple-element.8, f32[18,1024]{1,0:T(8,128)S(1)} %get-tuple-element.7, f32[18,1024]{1,0:T(8,128)S(1)} %get-tuple-element.9, f32[18,1024]{1,0:T(8,128)S(1)} %get-tuple-element.6), kind=kLoop, calls=%fused_computation | loop fusion | flops 73728 | bytes 442368 | tf_op jit(solution)/shard_map/sub | solution.py:426

commit v4 on v3

--- a/solution.py
+++ b/solution.py
@@ -52,12 +52,20 @@
     return jnp.concatenate(pieces, axis=0).astype(jnp.bfloat16)
 
 
+def as_column(row):
+    return jnp.broadcast_to(row, (LANES, LANES)).T
+
+
 def one_hot_low(index_row):
-    low = (index_row & (WIDE - 1)).astype(jnp.float32)
-    column = jnp.broadcast_to(low, (LANES, LANES)).T
+    column = as_column((index_row & (WIDE - 1)).astype(jnp.float32))
     lane = lax.broadcasted_iota(jnp.int32, (LANES, LANES), 1).astype(jnp.float32)
     halves = [jnp.where(column == lane + half * LANES, 1.0, 0.0) for half in range(2)]
     return jnp.concatenate(halves, axis=1).astype(jnp.bfloat16)
+
+
+def stacked(blocks):
+    pairs = [split_two(block) for block in blocks]
+    return jnp.concatenate([jnp.concatenate(pair, axis=0) for pair in pairs], axis=1).astype(jnp.bfloat16)
 
 
 def wide_dot(left, right):
@@ -68,9 +76,9 @@
     right_hbm, matrix_hbm, map_hbm, share_hbm, count_hbm, mass_hbm, absorb_hbm, imped_hbm,
     lead_ref, later_ref, along_ref, step_ref,
     right_ref, map_ref, share_ref, count_ref, mass_ref, absorb_ref, imped_ref, load_sem, meet_sem,
-    matrix, widened, field0, field1, image, diag, picked0, picked1, product, hot, hot_share,
-    out_buf, ghost_buf, part_buf, back_buf, sum_buf, sum_in,
-    matrix_sem, out_send, out_recv, part_send, part_recv, sum_send, sum_recv,
+    matrix, widened, field0, field1, image, diag, picked0, picked1, product, hot, hot_share, hot_back, match,
+    out_buf, ghost_buf, part_buf, back_buf, cross_buf, ghost_sum, list_out, list_in, sum_buf, sum_in,
+    matrix_sem, out_send, out_recv, part_send, part_recv, cross_send, cross_recv, list_send, list_recv, sum_send, sum_recv,
 ):
     me = lax.axis_index("dom")
     loads = [
@@ -100,6 +108,14 @@
 
     inside_to = [(me + o >= 0) & (me + o < N_DOM) for o in OFFSETS]
     inside_from = [(me - o >= 0) & (me - o < N_DOM) for o in OFFSETS]
+    crosses = sorted(
+        ((k, u) for k in range(4) for u in range(4) if k != u), key=lambda at: -abs(OFFSETS[at[1]] - OFFSETS[at[0]])
+    )
+
+    def cross_ok(k, u):
+        user = me - OFFSETS[k] + OFFSETS[u]
+        return inside_from[k] & (user >= 0) & (user < N_DOM)
+
 
     barrier = pltpu.get_barrier_semaphore()
     arrivals = jnp.int32(13)
@@ -132,6 +148,16 @@
         def _():
             for turn in range(2):
                 back_buf[turn, k] = jnp.zeros((ROWS, GH), jnp.float32)
+    for k, u in crosses:
+        @pl.when(jnp.logical_not(cross_ok(k, u)))
+        def _():
+            cross_buf[k, u, 0:TRACE] = jnp.zeros((TRACE, GH), jnp.float32)
+    for k in range(4):
+        @pl.when(jnp.logical_not(inside_from[k]))
+        def _():
+            list_in[k] = jnp.full((4, GH), -1.0, jnp.float32)
+        for u in range(4):
+            cross_buf[k, u, TRACE:ROWS] = jnp.zeros((ROWS - TRACE, GH), jnp.float32)
 
     lane = lax.broadcasted_iota(jnp.int32, (ROWS, GH), 1)
     alive = [lane < count_ref[0, k] for k in range(4)]
@@ -148,6 +174,20 @@
             device_id=(me + OFFSETS[k],), device_id_type=MESH,
         )
 
+    def list_copy(k):
+        return pltpu.make_async_remote_copy(
+            src_ref=list_out, dst_ref=list_in.at[k], send_sem=list_send.at[k], recv_sem=list_recv.at[k],
+            device_id=(me + OFFSETS[k],), device_id_type=MESH,
+        )
+
+    def cross_copy(k, u):
+        rows = pl.ds(0, TRACE)
+        return pltpu.make_async_remote_copy(
+            src_ref=part_buf.at[0, k, rows], dst_ref=cross_buf.at[u, k, rows],
+            send_sem=cross_send.at[u, k], recv_sem=cross_recv.at[u, k],
+            device_id=(me - OFFSETS[k] + OFFSETS[u],), device_id_type=MESH,
+        )
+
     def part_copy(turn, k):
         return pltpu.make_async_remote_copy(
             src_ref=part_buf.at[turn, k], dst_ref=back_buf.at[turn, k],
@@ -162,22 +202,38 @@
             out_buf[turn, k] = jnp.where(alive[k], gone, 0.0)
         if turn == 0:
             pl.semaphore_wait(barrier, arrivals)
-        for k in range(4):
+        for k in (0, 3, 1, 2):
             @pl.when(inside_to[k])
             def _():
                 out_copy(turn, k).start()
+                if turn == 0:
+                    list_copy(k).start()
 
     def await_out(turn):
         for k in range(4):
             @pl.when(inside_from[k])
             def _():
                 out_copy(turn, k).wait_recv()
+                if turn == 0:
+                    list_copy(k).wait_recv()
 
     def send_part(turn):
         for k in range(4):
             @pl.when(inside_from[k])
             def _():
                 part_copy(turn, k).start()
+
+    def send_cross():
+        for k, u in crosses:
+            @pl.when(cross_ok(k, u))
+            def _():
+                cross_copy(k, u).start()
+
+    def await_cross():
+        for k, u in crosses:
+            @pl.when(cross_ok(u, k))
+            def _():
+                cross_copy(k, u).wait_recv()
 
     def await_part(turn):
         for k in range(4):
@@ -192,17 +248,15 @@
                 cols = slice(b * LANES, (b + 1) * LANES)
                 picked[side, b] = lane_pick(blocks, map_ref[side:side + 1, cols], 0, None)
 
-    def pick_ghost(turn, picked, finish):
-        blocks = [lambda i, k=k: ghost_buf[turn, k, 8 * i:8 * i + 8] for k in range(4)]
+    def pick_ghost(ghosts, picked):
+        blocks = [lambda i, k=k: ghosts[k, 8 * i:8 * i + 8] for k in range(4)]
         for side in range(SIDES):
             for b in range(E_DEV // LANES):
                 cols = slice(b * LANES, (b + 1) * LANES)
                 base = lambda i, side=side, b=b: picked[side, b, 8 * i:8 * i + 8]
-                value = lane_pick(blocks, map_ref[side:side + 1, cols], F_DEV // LANES, base)
-                picked[side, b] = finish(side, b, value)
-
-    def multiply(picked):
-        energy = jnp.zeros((TRACE, LANES), jnp.float32)
+                picked[side, b] = lane_pick(blocks, map_ref[side:side + 1, cols], F_DEV // LANES, base)
+
+    def multiply(turn, picked):
         for b in range(E_DEV // LANES):
             cols = slice(b * LANES, (b + 1) * LANES)
 
@@ -214,10 +268,21 @@
 
             total = lax.fori_loop(0, SIDES, one, jnp.zeros((DOFS, LANES), jnp.float32))
             for side in range(SIDES):
-                piece = total[side * TRACE:(side + 1) * TRACE]
-                product[side, 0:TRACE, cols] = piece
-                energy = energy + piece * picked[side, b, 0:TRACE, :]
-        return jnp.sum(energy, axis=0, keepdims=True)
+                product[turn, side, 0:TRACE, cols] = total[side * TRACE:(side + 1) * TRACE]
+
+    def energy(step):
+        total = jnp.zeros((ROWS, LANES), jnp.float32)
+        for side in range(SIDES):
+            for b in range(E_DEV // LANES):
+                cols = slice(b * LANES, (b + 1) * LANES)
+                image_part = product[0, side, :, cols]
+                value = picked0[side, b]
+                if step is not None:
+                    image_part = image_part - step * product[1, side, :, cols]
+                    product[1, side, :, cols] = image_part
+                    value = value - step * picked1[side, b]
+                total = total + value * image_part
+        return jnp.sum(total, axis=0, keepdims=True)
 
     def face_sums(ref):
         square = jnp.zeros((8, LANES), jnp.float32)
@@ -230,22 +295,22 @@
             weighted = weighted + both * diag[b:b + 1, :]
         return jnp.sum(square, axis=0, keepdims=True), jnp.sum(weighted, axis=0, keepdims=True)
 
-    def scatter(groups):
+    def scatter(turn, groups):
         total = jnp.zeros((len(groups) * 2 * ROWS, WIDE), jnp.float32)
         for side in range(SIDES):
-            left = spread_rows(product[side], map_ref[side:side + 1, :], groups)
+            left = spread_rows(product[turn, side], map_ref[side:side + 1, :], groups)
             total = total + wide_dot(left, hot[side * E_DEV:(side + 1) * E_DEV, :])
         for at in range(len(groups)):
             base = at * 2 * ROWS
             yield total[base:base + ROWS] + total[base + ROWS:base + 2 * ROWS]
 
     def scatter_ghost(turn):
-        for at, both in enumerate(scatter((4, 5))):
+        for at, both in enumerate(scatter(turn, (4, 5))):
             part_buf[turn, 2 * at] = both[:, 0:GH]
             part_buf[turn, 2 * at + 1] = both[:, GH:]
 
     def scatter_own(turn, ref):
-        for at, both in enumerate(scatter((0, 1, 2, 3))):
+        for at, both in enumerate(scatter(turn, (0, 1, 2, 3))):
             for half in range(2):
                 b = 2 * at + half
                 cols = slice(b * LANES, (b + 1) * LANES)
@@ -296,9 +361,27 @@
         return first, second
 
     def clear_tail(ref):
+        for turn in range(2):
+            for side in range(SIDES):
+                ref[turn, side, TRACE:ROWS, :] = jnp.zeros((ROWS - TRACE, E_DEV), jnp.float32)
+
+    def complete_ghosts():
+        for k in range(4):
+            left = stacked([part_buf[0, k] if u == k else cross_buf[k, u] for u in range(4)])
+            both = wide_dot(left, match[k])
+            ghost_sum[k] = ghost_buf[1, k] + both[0:ROWS] + both[ROWS:2 * ROWS]
+
+    def pick_back():
+        both = wide_dot(stacked([back_buf[0, k] for k in range(4)]), hot_back[...])
         for side in range(SIDES):
-            ref[side, TRACE:ROWS, :] = jnp.zeros((ROWS - TRACE, E_DEV), jnp.float32)
-
+            for b in range(E_DEV // LANES):
+                first = side * E_DEV + b * LANES
+                part = both[0:ROWS, first:first + LANES] + both[ROWS:2 * ROWS, first:first + LANES]
+                picked1[side, b] = picked1[side, b] + part
+
+    lists = [jnp.where(alive[k][0:1], share_ref[k:k + 1, :].astype(jnp.float32), -1.0) for k in range(4)]
+    for k in range(4):
+        list_out[k:k + 1, :] = lists[k]
     send_out(0, field0)
     meet(0, line_y)
     clear_tail(product)
@@ -309,6 +392,14 @@
     for k in range(4):
         hot_share[k * GH:(k + 1) * GH, :] = one_hot_low(share_ref[k:k + 1, :])
     square, weighted = face_sums(field0)
+    for u in range(4):
+        column = as_column(lists[u])
+        for side in range(SIDES):
+            for b in range(E_DEV // LANES):
+                cols = slice(b * LANES, (b + 1) * LANES)
+                hit = column == map_ref[side:side + 1, cols].astype(jnp.float32)
+                first = side * E_DEV + b * LANES
+                hot_back[u * GH:(u + 1) * GH, first:first + LANES] = jnp.where(hit, 1.0, 0.0).astype(jnp.bfloat16)
     pl.semaphore_wait(meet_sem.at[0], 3)
     meet(1, line_z)
     matrix_copy.wait()
@@ -324,25 +415,35 @@
     pl.semaphore_wait(meet_sem.at[1], 3)
     await_out(0)
 
-    pick_ghost(0, picked0, lambda side, b, value: value)
-    weighted = weighted + multiply(picked0)
+    pick_ghost(ghost_buf.at[0], picked0)
+    multiply(0, picked0)
     scatter_ghost(0)
+    send_cross()
     send_part(0)
-    sum_start(0, square, weighted)
     scatter_own(0, field0)
+    send_out(1, image.at[0])
+    sum_start(0, square, weighted + energy(None))
+    pick_own(image.at[0], picked1)
+    for k in range(4):
+        target = jnp.where(list_in[k, k:k + 1, :] < 0.0, -2.0, list_in[k, k:k + 1, :])
+        for u in range(4):
+            hit = as_column(list_in[k, u:u + 1, :]) == target
+            match[k, u * GH:(u + 1) * GH, :] = jnp.where(hit, 1.0, 0.0).astype(jnp.bfloat16)
     await_part(0)
+    await_out(1)
+    await_cross()
+    complete_ghosts()
+    pick_back()
     add_back(0)
-    send_out(1, image.at[0])
-    pick_own(image.at[0], picked1)
+    pick_ghost(ghost_sum, picked1)
+    multiply(1, picked1)
     norm0, curve0 = sum_finish(0)
     step0 = norm0 / curve0
     for b in range(F_DEV // LANES):
         cols = slice(b * LANES, (b + 1) * LANES)
         field1[:, cols] = field0[:, cols] - step0 * image[0, :, cols]
     square, weighted = face_sums(field1)
-    await_out(1)
-    pick_ghost(1, picked1, lambda side, b, value: picked0[side, b] - step0 * value)
-    sum_start(1, square, weighted + multiply(picked1))
+    sum_start(1, square, weighted + energy(step0))
     scatter_ghost(1)
     send_part(1)
     scatter_own(1, field1)
@@ -364,10 +465,16 @@
             @pl.when(inside_to[k])
             def _():
                 out_copy(turn, k).wait_send()
+                if turn == 0:
+                    list_copy(k).wait_send()
             @pl.when(inside_from[k])
             def _():
                 part_copy(turn, k).wait_send()
         sum_whole(turn, sum_send).wait()
+    for k, u in crosses:
+        @pl.when(cross_ok(k, u))
+        def _():
+            cross_copy(k, u).wait_send()
 
 
 def shards(right_side, element_matrix, face_map, share_index, share_count, face_mass, absorbing, impedance):
@@ -399,13 +506,19 @@
             pltpu.VMEM((8, LANES), f32),
             pltpu.VMEM((SIDES, 4, ROWS, LANES), f32),
             pltpu.VMEM((SIDES, 4, ROWS, LANES), f32),
-            pltpu.VMEM((SIDES, ROWS, E_DEV), f32),
+            pltpu.VMEM((2, SIDES, ROWS, E_DEV), f32),
             pltpu.VMEM((SIDES * E_DEV, WIDE), bf16),
             pltpu.VMEM((4 * GH, WIDE), bf16),
+            pltpu.VMEM((4 * GH, SIDES * E_DEV), bf16),
+            pltpu.VMEM((4, 4 * GH, GH), bf16),
             pltpu.VMEM((2, 4, ROWS, GH), f32),
             pltpu.VMEM((2, 4, ROWS, GH), f32),
             pltpu.VMEM((2, 4, ROWS, GH), f32),
             pltpu.VMEM((2, 4, ROWS, GH), f32),
+            pltpu.VMEM((4, 4, ROWS, GH), f32),
+            pltpu.VMEM((4, ROWS, GH), f32),
+            pltpu.VMEM((4, GH), f32),
+            pltpu.VMEM((4, 4, GH), f32),
             pltpu.VMEM((2, 1, LANES), f32),
             pltpu.VMEM((2, N_DOM, 1, LANES), f32),
             pltpu.SemaphoreType.DMA,
@@ -413,6 +526,10 @@
             pltpu.SemaphoreType.DMA((2, 4)),
             pltpu.SemaphoreType.DMA((2, 4)),
             pltpu.SemaphoreType.DMA((2, 4)),
+            pltpu.SemaphoreType.DMA((4, 4)),
+            pltpu.SemaphoreType.DMA((4, 4)),
+            pltpu.SemaphoreType.DMA((4,)),
+            pltpu.SemaphoreType.DMA((4,)),
             pltpu.SemaphoreType.DMA((2,)),
             pltpu.SemaphoreType.DMA((2,)),
         ],

time: 34 us -> 29.7 us (0.87)
  Pallas kernels: 32.6 us -> 28.3 us
    pallas_call x1, Pallas kernels: 32.6 us -> 28.3 us  [shards(): pl.pallas_call(kernel, name='trace_cg', out_shape=(out, out, out, out), i...]
where the time goes in v4:
time: 29.7 us; the launch traced here: 29.6 us
  Pallas kernels  28.3 us (95%)
  other arithmetic  0.7 us (2%)
  between operations  0.64 us (2%)
    pallas_call x1, Pallas kernels, shards(): pl.pallas_call(kernel, name='trace_cg', out_shape=(out, out, out, out), i...  28.3 us
    sub x1, other arithmetic, shards(): return (lead + step * later, later - step * along)  0.7 us

profile of v4, /device:TPU:1, one launch (start us, length us, event | category | flops | bytes accessed | tf_op | source)
XLA Modules:
  0.0 29.6 jit_solution(6976146926036479599)
XLA Ops:
  0.6 28.3 %trace_cg.1 = (f32[18,1024]{1,0:T(8,128)S(1)}, f32[18,1024]{1,0:T(8,128)S(1)}, f32[18,1024]{1,0:T(8,128)S(1)}, f32[18,1024]{1,0:T(8,128)S(1)}) custom-call(f32[18,1024]{1,0:T(8,128)} %right_hbm.1, bf16[72,72,512]{2,1,0:T(8,128)(2,1)} %matrix_hbm.1, s32[4,512]{1,0:T(4,128)} %map_hbm.1, s32[4,128]{1,0:T(4,128)} %bitcast.7, s32[1,4]{1,0:T(1,128)} %count_hbm.1, ...), custom_call_target="tpu_custom_call" | custom-call | tf_op jit(solution)/shard_map/trace_cg/pallas_call | solution.py:485
  28.9 0.7 %multiply_subtract_fusion = (f32[18,1024]{1,0:T(8,128)}, f32[18,1024]{1,0:T(8,128)}) fusion(f32[18,1024]{1,0:T(8,128)S(1)} %get-tuple-element.8, f32[18,1024]{1,0:T(8,128)S(1)} %get-tuple-element.7, f32[18,1024]{1,0:T(8,128)S(1)} %get-tuple-element.9, f32[18,1024]{1,0:T(8,128)S(1)} %get-tuple-element.6), kind=kLoop, calls=%fused_computation | loop fusion | flops 73728 | bytes 442368 | tf_op jit(solution)/shard_map/sub | solution.py:543

commit v5 on v4

--- a/solution.py
+++ b/solution.py
@@ -77,8 +77,8 @@
     lead_ref, later_ref, along_ref, step_ref,
     right_ref, map_ref, share_ref, count_ref, mass_ref, absorb_ref, imped_ref, load_sem, meet_sem,
     matrix, widened, field0, field1, image, diag, picked0, picked1, product, hot, hot_share, hot_back, match,
-    out_buf, ghost_buf, part_buf, back_buf, cross_buf, ghost_sum, list_out, list_in, sum_buf, sum_in,
-    matrix_sem, out_send, out_recv, part_send, part_recv, cross_send, cross_recv, list_send, list_recv, sum_send, sum_recv,
+    out_buf, ghost_in, part_buf, back_in, near_in, ghost_sum, list_out, list_in, sum_buf, sum_in,
+    matrix_sem, trade_send, trade_recv, list_send, list_recv, sum_send, sum_recv,
 ):
     me = lax.axis_index("dom")
     loads = [
@@ -88,6 +88,15 @@
             (mass_hbm, mass_ref), (absorb_hbm, absorb_ref), (imped_hbm, imped_ref),
         ))
     ]
+    rows18 = pl.ds(0, TRACE)
+
+    def blocks_wait(ref, sem, count, options):
+        for n in options:
+            @pl.when(count == n)
+            def _(n=n):
+                some = ref.at[pl.ds(0, n), rows18]
+                pltpu.make_async_copy(some, some, sem).wait()
+
     for load in loads:
         load.start()
     matrix_copy = pltpu.make_async_copy(matrix_hbm, matrix, matrix_sem)
@@ -116,6 +125,12 @@
         user = me - OFFSETS[k] + OFFSETS[u]
         return inside_from[k] & (user >= 0) & (user < N_DOM)
 
+
+    def tally(flags):
+        return functools.reduce(lambda total, flag: total + flag.astype(jnp.int32), flags, jnp.int32(0))
+
+    near_to, near_from = tally(inside_to), tally(inside_from)
+    all_near = near_to + near_from + tally([cross_ok(k, u) for k, u in crosses])
 
     barrier = pltpu.get_barrier_semaphore()
     arrivals = jnp.int32(13)
@@ -139,25 +154,25 @@
     field0[0:TRACE, :] = right_ref[...]
     field0[TRACE:ROWS, :] = jnp.zeros((ROWS - TRACE, F_DEV), jnp.float32)
     diag[...] = mass_ref[...] + absorb_ref[...].astype(jnp.float32) * imped_ref[...]
+    blank = jnp.zeros((TRACE, GH), jnp.float32)
     for k in range(4):
         @pl.when(jnp.logical_not(inside_from[k]))
         def _():
-            for turn in range(2):
-                ghost_buf[turn, k] = jnp.zeros((ROWS, GH), jnp.float32)
+            ghost_in[k, 0:TRACE] = blank
+            near_in[4 + k, 0:TRACE] = blank
+            list_in[k] = jnp.full((4, GH), -1.0, jnp.float32)
         @pl.when(jnp.logical_not(inside_to[k]))
         def _():
-            for turn in range(2):
-                back_buf[turn, k] = jnp.zeros((ROWS, GH), jnp.float32)
+            near_in[k, 0:TRACE] = blank
+            back_in[k, 0:TRACE] = blank
+        for ref in (ghost_in, back_in):
+            ref[k, TRACE:ROWS] = jnp.zeros((ROWS - TRACE, GH), jnp.float32)
     for k, u in crosses:
         @pl.when(jnp.logical_not(cross_ok(k, u)))
         def _():
-            cross_buf[k, u, 0:TRACE] = jnp.zeros((TRACE, GH), jnp.float32)
-    for k in range(4):
-        @pl.when(jnp.logical_not(inside_from[k]))
-        def _():
-            list_in[k] = jnp.full((4, GH), -1.0, jnp.float32)
-        for u in range(4):
-            cross_buf[k, u, TRACE:ROWS] = jnp.zeros((ROWS - TRACE, GH), jnp.float32)
+            near_in[8 + 4 * k + u, 0:TRACE] = blank
+    for at in range(24):
+        near_in[at, TRACE:ROWS] = jnp.zeros((ROWS - TRACE, GH), jnp.float32)
 
     lane = lax.broadcasted_iota(jnp.int32, (ROWS, GH), 1)
     alive = [lane < count_ref[0, k] for k in range(4)]
@@ -167,33 +182,47 @@
             lambda i, b=b: ref[8 * i:8 * i + 8, b * LANES:(b + 1) * LANES] for b in range(F_DEV // LANES)
         ]
 
+    def trade(turn, source, target, other):
+        return pltpu.make_async_remote_copy(
+            src_ref=source.at[rows18], dst_ref=target.at[rows18],
+            send_sem=trade_send.at[turn], recv_sem=trade_recv.at[turn], device_id=(other,), device_id_type=MESH,
+        )
+
     def out_copy(turn, k):
+        return trade(turn, out_buf.at[turn, k], ghost_in.at[k] if turn == 0 else near_in.at[4 + k], me + OFFSETS[k])
+
+    def list_copy(k):
         return pltpu.make_async_remote_copy(
-            src_ref=out_buf.at[turn, k], dst_ref=ghost_buf.at[turn, k],
-            send_sem=out_send.at[turn, k], recv_sem=out_recv.at[turn, k],
+            src_ref=list_out, dst_ref=list_in.at[k], send_sem=list_send, recv_sem=list_recv,
             device_id=(me + OFFSETS[k],), device_id_type=MESH,
         )
 
-    def list_copy(k):
-        return pltpu.make_async_remote_copy(
-            src_ref=list_out, dst_ref=list_in.at[k], send_sem=list_send.at[k], recv_sem=list_recv.at[k],
-            device_id=(me + OFFSETS[k],), device_id_type=MESH,
-        )
+    def lists_wait(sem, count):
+        for n in (2, 3, 4):
+            @pl.when(count == n)
+            def _(n=n):
+                some = list_in.at[pl.ds(0, n)]
+                pltpu.make_async_copy(some, some, sem).wait()
 
     def cross_copy(k, u):
-        rows = pl.ds(0, TRACE)
-        return pltpu.make_async_remote_copy(
-            src_ref=part_buf.at[0, k, rows], dst_ref=cross_buf.at[u, k, rows],
-            send_sem=cross_send.at[u, k], recv_sem=cross_recv.at[u, k],
-            device_id=(me - OFFSETS[k] + OFFSETS[u],), device_id_type=MESH,
-        )
+        return trade(1, part_buf.at[0, k], near_in.at[8 + 4 * u + k], me - OFFSETS[k] + OFFSETS[u])
 
     def part_copy(turn, k):
-        return pltpu.make_async_remote_copy(
-            src_ref=part_buf.at[turn, k], dst_ref=back_buf.at[turn, k],
-            send_sem=part_send.at[turn, k], recv_sem=part_recv.at[turn, k],
-            device_id=(me - OFFSETS[k],), device_id_type=MESH,
-        )
+        return trade(1 + turn, part_buf.at[turn, k], near_in.at[k] if turn == 0 else back_in.at[k], me - OFFSETS[k])
+
+    trades = (
+        (ghost_in, near_to, near_from, (2, 3, 4)),
+        (near_in, all_near, all_near, (9, 13, 17, 19, 20)),
+        (back_in, near_from, near_to, (2, 3, 4)),
+    )
+
+    def trade_wait_recv(turn):
+        ref, _, count, options = trades[turn]
+        blocks_wait(ref, trade_recv.at[turn], count, options)
+
+    def trade_wait_send(turn):
+        ref, count, _, options = trades[turn]
+        blocks_wait(ref, trade_send.at[turn], count, options)
 
     def send_out(turn, ref):
         blocks = own_blocks(ref)
@@ -209,14 +238,6 @@
                 if turn == 0:
                     list_copy(k).start()
 
-    def await_out(turn):
-        for k in range(4):
-            @pl.when(inside_from[k])
-            def _():
-                out_copy(turn, k).wait_recv()
-                if turn == 0:
-                    list_copy(k).wait_recv()
-
     def send_part(turn):
         for k in range(4):
             @pl.when(inside_from[k])
@@ -228,18 +249,6 @@
             @pl.when(cross_ok(k, u))
             def _():
                 cross_copy(k, u).start()
-
-    def await_cross():
-        for k, u in crosses:
-            @pl.when(cross_ok(u, k))
-            def _():
-                cross_copy(k, u).wait_recv()
-
-    def await_part(turn):
-        for k in range(4):
-            @pl.when(inside_to[k])
-            def _():
-                part_copy(turn, k).wait_recv()
 
     def pick_own(ref, picked):
         blocks = own_blocks(ref)
@@ -316,10 +325,10 @@
                 cols = slice(b * LANES, (b + 1) * LANES)
                 image[turn, :, cols] = both[:, half * LANES:(half + 1) * LANES] + diag[b:b + 1, :] * ref[:, cols]
 
-    def add_back(turn):
+    def add_back(turn, back):
         total = jnp.zeros((4 * 2 * ROWS, WIDE), jnp.float32)
         for k in range(4):
-            value = jnp.where(alive[k], back_buf[turn, k], 0.0)
+            value = jnp.where(alive[k], back[k], 0.0)
             left = spread_rows(value, share_ref[k:k + 1, :], (0, 1, 2, 3))
             total = total + wide_dot(left, hot_share[k * GH:(k + 1) * GH, :])
         for group in range(4):
@@ -343,17 +352,14 @@
         for at in others:
             pltpu.make_async_remote_copy(
                 src_ref=sum_buf.at[turn], dst_ref=sum_in.at[turn, me],
-                send_sem=sum_send.at[turn], recv_sem=sum_recv.at[turn],
+                send_sem=sum_send, recv_sem=sum_recv.at[turn],
                 device_id=(device_at(*at),), device_id_type=MESH,
             ).start()
 
-    def sum_whole(turn, sem):
-        return pltpu.make_async_copy(
-            sum_in.at[turn, pl.ds(0, N_DOM - 1)], sum_in.at[turn, pl.ds(1, N_DOM - 1)], sem.at[turn]
-        )
-
     def sum_finish(turn):
-        sum_whole(turn, sum_recv).wait()
+        pltpu.make_async_copy(
+            sum_in.at[turn, pl.ds(0, N_DOM - 1)], sum_in.at[turn, pl.ds(1, N_DOM - 1)], sum_recv.at[turn]
+        ).wait()
         total = jnp.sum(sum_in[turn], axis=0)
         lane_at = lax.broadcasted_iota(jnp.int32, (1, LANES), 1)
         first = jnp.sum(jnp.where(lane_at < LANES // 2, total, 0.0), axis=1, keepdims=True)
@@ -367,12 +373,12 @@
 
     def complete_ghosts():
         for k in range(4):
-            left = stacked([part_buf[0, k] if u == k else cross_buf[k, u] for u in range(4)])
+            left = stacked([part_buf[0, k] if u == k else near_in[8 + 4 * k + u] for u in range(4)])
             both = wide_dot(left, match[k])
-            ghost_sum[k] = ghost_buf[1, k] + both[0:ROWS] + both[ROWS:2 * ROWS]
+            ghost_sum[k] = near_in[4 + k] + both[0:ROWS] + both[ROWS:2 * ROWS]
 
     def pick_back():
-        both = wide_dot(stacked([back_buf[0, k] for k in range(4)]), hot_back[...])
+        both = wide_dot(stacked([near_in[k] for k in range(4)]), hot_back[...])
         for side in range(SIDES):
             for b in range(E_DEV // LANES):
                 first = side * E_DEV + b * LANES
@@ -413,9 +419,10 @@
     pick_own(field0, picked0)
     lax.fori_loop(0, DOFS, widen, 0, unroll=2)
     pl.semaphore_wait(meet_sem.at[1], 3)
-    await_out(0)
-
-    pick_ghost(ghost_buf.at[0], picked0)
+    trade_wait_recv(0)
+    lists_wait(list_recv, near_from)
+
+    pick_ghost(ghost_in, picked0)
     multiply(0, picked0)
     scatter_ghost(0)
     send_cross()
@@ -429,12 +436,10 @@
         for u in range(4):
             hit = as_column(list_in[k, u:u + 1, :]) == target
             match[k, u * GH:(u + 1) * GH, :] = jnp.where(hit, 1.0, 0.0).astype(jnp.bfloat16)
-    await_part(0)
-    await_out(1)
-    await_cross()
+    trade_wait_recv(1)
     complete_ghosts()
     pick_back()
-    add_back(0)
+    add_back(0, near_in)
     pick_ghost(ghost_sum, picked1)
     multiply(1, picked1)
     norm0, curve0 = sum_finish(0)
@@ -447,8 +452,8 @@
     scatter_ghost(1)
     send_part(1)
     scatter_own(1, field1)
-    await_part(1)
-    add_back(1)
+    trade_wait_recv(2)
+    add_back(1, back_in)
     norm1, curve1 = sum_finish(1)
     ratio = norm1 / norm0
     step1 = norm1 / (curve1 - ratio * norm1 / step0)
@@ -460,21 +465,12 @@
         along_ref[:, cols] = image[1, 0:TRACE, cols] + ratio * image[0, 0:TRACE, cols]
     step_ref[...] = jnp.broadcast_to(step1, (TRACE, F_DEV))
 
-    for turn in range(2):
-        for k in range(4):
-            @pl.when(inside_to[k])
-            def _():
-                out_copy(turn, k).wait_send()
-                if turn == 0:
-                    list_copy(k).wait_send()
-            @pl.when(inside_from[k])
-            def _():
-                part_copy(turn, k).wait_send()
-        sum_whole(turn, sum_send).wait()
-    for k, u in crosses:
-        @pl.when(cross_ok(k, u))
-        def _():
-            cross_copy(k, u).wait_send()
+    for turn in range(3):
+        trade_wait_send(turn)
+    lists_wait(list_send, near_to)
+    pltpu.make_async_copy(
+        sum_in.at[:, pl.ds(0, N_DOM - 1)], sum_in.at[:, pl.ds(1, N_DOM - 1)], sum_send
+    ).wait()
 
 
 def shards(right_side, element_matrix, face_map, share_index, share_count, face_mass, absorbing, impedance):
@@ -512,25 +508,21 @@
             pltpu.VMEM((4 * GH, SIDES * E_DEV), bf16),
             pltpu.VMEM((4, 4 * GH, GH), bf16),
             pltpu.VMEM((2, 4, ROWS, GH), f32),
+            pltpu.VMEM((4, ROWS, GH), f32),
             pltpu.VMEM((2, 4, ROWS, GH), f32),
-            pltpu.VMEM((2, 4, ROWS, GH), f32),
-            pltpu.VMEM((2, 4, ROWS, GH), f32),
-            pltpu.VMEM((4, 4, ROWS, GH), f32),
+            pltpu.VMEM((4, ROWS, GH), f32),
+            pltpu.VMEM((24, ROWS, GH), f32),
             pltpu.VMEM((4, ROWS, GH), f32),
             pltpu.VMEM((4, GH), f32),
             pltpu.VMEM((4, 4, GH), f32),
             pltpu.VMEM((2, 1, LANES), f32),
             pltpu.VMEM((2, N_DOM, 1, LANES), f32),
             pltpu.SemaphoreType.DMA,
-            pltpu.SemaphoreType.DMA((2, 4)),
-            pltpu.SemaphoreType.DMA((2, 4)),
-            pltpu.SemaphoreType.DMA((2, 4)),
-            pltpu.SemaphoreType.DMA((2, 4)),
-            pltpu.SemaphoreType.DMA((4, 4)),
-            pltpu.SemaphoreType.DMA((4, 4)),
-            pltpu.SemaphoreType.DMA((4,)),
-            pltpu.SemaphoreType.DMA((4,)),
-            pltpu.SemaphoreType.DMA((2,)),
+            pltpu.SemaphoreType.DMA((3,)),
+            pltpu.SemaphoreType.DMA((3,)),
+            pltpu.SemaphoreType.DMA,
+            pltpu.SemaphoreType.DMA,
+            pltpu.SemaphoreType.DMA,
             pltpu.SemaphoreType.DMA((2,)),
         ],
         compiler_params=pltpu.CompilerParams(

time: 29.7 us -> 28.9 us (0.973)
  Pallas kernels: 28.3 us -> 27.5 us
    pallas_call x1, Pallas kernels: 28.3 us -> 27.5 us  [shards(): pl.pallas_call(kernel, name='trace_cg', out_shape=(out, out, out, out), i...]
where the time goes in v5:
time: 28.9 us; the launch traced here: 28.8 us
  Pallas kernels  27.5 us (95%)
  other arithmetic  0.7 us (2%)
  between operations  0.64 us (2%)
    pallas_call x1, Pallas kernels, shards(): pl.pallas_call(kernel, name='trace_cg', out_shape=(out, out, out, out), i...  27.5 us
    sub x1, other arithmetic, shards(): return (lead + step * later, later - step * along)  0.7 us

profile of v5, /device:TPU:1, one launch (start us, length us, event | category | flops | bytes accessed | tf_op | source)
XLA Modules:
  0.0 28.8 jit_solution(16767017763998174093)
XLA Ops:
  0.6 27.5 %trace_cg.1 = (f32[18,1024]{1,0:T(8,128)S(1)}, f32[18,1024]{1,0:T(8,128)S(1)}, f32[18,1024]{1,0:T(8,128)S(1)}, f32[18,1024]{1,0:T(8,128)S(1)}) custom-call(f32[18,1024]{1,0:T(8,128)} %right_hbm.1, bf16[72,72,512]{2,1,0:T(8,128)(2,1)} %matrix_hbm.1, s32[4,512]{1,0:T(4,128)} %map_hbm.1, s32[4,128]{1,0:T(4,128)} %bitcast.7, s32[1,4]{1,0:T(1,128)} %count_hbm.1, ...), custom_call_target="tpu_custom_call" | custom-call | tf_op jit(solution)/shard_map/trace_cg/pallas_call | solution.py:481
  28.1 0.7 %multiply_subtract_fusion = (f32[18,1024]{1,0:T(8,128)}, f32[18,1024]{1,0:T(8,128)}) fusion(f32[18,1024]{1,0:T(8,128)S(1)} %get-tuple-element.8, f32[18,1024]{1,0:T(8,128)S(1)} %get-tuple-element.7, f32[18,1024]{1,0:T(8,128)S(1)} %get-tuple-element.9, f32[18,1024]{1,0:T(8,128)S(1)} %get-tuple-element.6), kind=kLoop, calls=%fused_computation | loop fusion | flops 73728 | bytes 442368 | tf_op jit(solution)/shard_map/sub | solution.py:535

commit v6 on v5

--- a/solution.py
+++ b/solution.py
@@ -76,7 +76,7 @@
     right_hbm, matrix_hbm, map_hbm, share_hbm, count_hbm, mass_hbm, absorb_hbm, imped_hbm,
     lead_ref, later_ref, along_ref, step_ref,
     right_ref, map_ref, share_ref, count_ref, mass_ref, absorb_ref, imped_ref, load_sem, meet_sem,
-    matrix, widened, field0, field1, image, diag, picked0, picked1, product, hot, hot_share, hot_back, match,
+    matrix, widened, field0, field1, image, diag, picked0, picked1, product, hot, hot_share, hot_back, back_left, match,
     out_buf, ghost_in, part_buf, back_in, near_in, ghost_sum, list_out, list_in, sum_buf, sum_in,
     matrix_sem, trade_send, trade_recv, list_send, list_recv, sum_send, sum_recv,
 ):
@@ -97,11 +97,6 @@
                 some = ref.at[pl.ds(0, n), rows18]
                 pltpu.make_async_copy(some, some, sem).wait()
 
-    for load in loads:
-        load.start()
-    matrix_copy = pltpu.make_async_copy(matrix_hbm, matrix, matrix_sem)
-    matrix_copy.start()
-
     core = lax.rem(me, 2)
     at_x = lax.rem(me // 2, 4)
     at_y = lax.rem(me // 8, 4)
@@ -144,6 +139,12 @@
     pairs_x = [device_at(0, 0, d, c) for d in range(4) for c in range(2) if d or c]
     for other in pairs_x + line_y + line_z:
         pl.semaphore_signal(barrier, inc=1, device_id=(other,), device_id_type=MESH)
+
+    for load in loads:
+        load.start()
+    matrix_copy = pltpu.make_async_copy(matrix_hbm, matrix, matrix_sem)
+    matrix_copy.start()
+
 
     def meet(at, others):
         for other in others:
@@ -257,38 +258,43 @@
                 cols = slice(b * LANES, (b + 1) * LANES)
                 picked[side, b] = lane_pick(blocks, map_ref[side:side + 1, cols], 0, None)
 
-    def pick_ghost(ghosts, picked):
+    def pick_ghost(ghosts, picked, b):
         blocks = [lambda i, k=k: ghosts[k, 8 * i:8 * i + 8] for k in range(4)]
-        for side in range(SIDES):
-            for b in range(E_DEV // LANES):
-                cols = slice(b * LANES, (b + 1) * LANES)
-                base = lambda i, side=side, b=b: picked[side, b, 8 * i:8 * i + 8]
-                picked[side, b] = lane_pick(blocks, map_ref[side:side + 1, cols], F_DEV // LANES, base)
-
-    def multiply(turn, picked):
-        for b in range(E_DEV // LANES):
-            cols = slice(b * LANES, (b + 1) * LANES)
-
-            def one(side, total, b=b):
-                for c in range(TRACE):
-                    row = picked[side, b, c:c + 1, :]
-                    total = total + widened[b, side * TRACE + c] * row
-                return total
-
-            total = lax.fori_loop(0, SIDES, one, jnp.zeros((DOFS, LANES), jnp.float32))
-            for side in range(SIDES):
-                product[turn, side, 0:TRACE, cols] = total[side * TRACE:(side + 1) * TRACE]
+        first = b * LANES if isinstance(b, int) else pl.multiple_of(b * LANES, LANES)
+        cols = pl.ds(first, LANES)
+        for side in range(SIDES):
+            base = lambda i, side=side: picked[side, b, 8 * i:8 * i + 8]
+            picked[side, b] = lane_pick(blocks, map_ref[side:side + 1, cols], F_DEV // LANES, base)
+
+    def multiply(turn, picked, b):
+        def one(side, total):
+            for c in range(TRACE):
+                row = picked[side, b, c:c + 1, :]
+                total = total + widened[b, side * TRACE + c] * row
+            return total
+
+        total = jnp.zeros((DOFS, LANES), jnp.float32)
+        for side in range(SIDES):
+            total = one(side, total)
+        for side in range(SIDES):
+            product[turn, side, b, 0:TRACE, :] = total[side * TRACE:(side + 1) * TRACE]
+
+    def scatter_block(turn, groups, b):
+        lefts = [
+            spread_rows(product[turn, side, b], map_ref[side:side + 1, b * LANES:(b + 1) * LANES], groups)
+            for side in range(SIDES)
+        ]
+        return wide_dot(jnp.concatenate(lefts, axis=1), hot[b])
 
     def energy(step):
         total = jnp.zeros((ROWS, LANES), jnp.float32)
         for side in range(SIDES):
             for b in range(E_DEV // LANES):
-                cols = slice(b * LANES, (b + 1) * LANES)
-                image_part = product[0, side, :, cols]
+                image_part = product[0, side, b]
                 value = picked0[side, b]
                 if step is not None:
-                    image_part = image_part - step * product[1, side, :, cols]
-                    product[1, side, :, cols] = image_part
+                    image_part = image_part - step * product[1, side, b]
+                    product[1, side, b] = image_part
                     value = value - step * picked1[side, b]
                 total = total + value * image_part
         return jnp.sum(total, axis=0, keepdims=True)
@@ -304,22 +310,21 @@
             weighted = weighted + both * diag[b:b + 1, :]
         return jnp.sum(square, axis=0, keepdims=True), jnp.sum(weighted, axis=0, keepdims=True)
 
-    def scatter(turn, groups):
-        total = jnp.zeros((len(groups) * 2 * ROWS, WIDE), jnp.float32)
-        for side in range(SIDES):
-            left = spread_rows(product[turn, side], map_ref[side:side + 1, :], groups)
-            total = total + wide_dot(left, hot[side * E_DEV:(side + 1) * E_DEV, :])
+    def scatter(turn, groups, total):
+        if total is None:
+            parts = [scatter_block(turn, groups, b) for b in range(E_DEV // LANES)]
+            total = (parts[0] + parts[1]) + (parts[2] + parts[3])
         for at in range(len(groups)):
             base = at * 2 * ROWS
             yield total[base:base + ROWS] + total[base + ROWS:base + 2 * ROWS]
 
-    def scatter_ghost(turn):
-        for at, both in enumerate(scatter(turn, (4, 5))):
+    def scatter_ghost(turn, total=None):
+        for at, both in enumerate(scatter(turn, (4, 5), total)):
             part_buf[turn, 2 * at] = both[:, 0:GH]
             part_buf[turn, 2 * at + 1] = both[:, GH:]
 
     def scatter_own(turn, ref):
-        for at, both in enumerate(scatter(turn, (0, 1, 2, 3))):
+        for at, both in enumerate(scatter(turn, (0, 1, 2, 3), None)):
             for half in range(2):
                 b = 2 * at + half
                 cols = slice(b * LANES, (b + 1) * LANES)
@@ -348,10 +353,10 @@
         second = second + pltpu.roll(second, LANES // 2, 1)
         row = jnp.where(lane_at < LANES // 2, first, second)
         sum_buf[turn] = row
-        sum_in[turn, me] = row
+        sum_in[turn, pl.ds(me, 1), :] = row
         for at in others:
             pltpu.make_async_remote_copy(
-                src_ref=sum_buf.at[turn], dst_ref=sum_in.at[turn, me],
+                src_ref=sum_buf.at[turn], dst_ref=sum_in.at[turn, pl.ds(me, 1), :],
                 send_sem=sum_send, recv_sem=sum_recv.at[turn],
                 device_id=(device_at(*at),), device_id_type=MESH,
             ).start()
@@ -360,7 +365,7 @@
         pltpu.make_async_copy(
             sum_in.at[turn, pl.ds(0, N_DOM - 1)], sum_in.at[turn, pl.ds(1, N_DOM - 1)], sum_recv.at[turn]
         ).wait()
-        total = jnp.sum(sum_in[turn], axis=0)
+        total = jnp.sum(sum_in[turn], axis=0, keepdims=True)
         lane_at = lax.broadcasted_iota(jnp.int32, (1, LANES), 1)
         first = jnp.sum(jnp.where(lane_at < LANES // 2, total, 0.0), axis=1, keepdims=True)
         second = jnp.sum(jnp.where(lane_at < LANES // 2, 0.0, total), axis=1, keepdims=True)
@@ -369,7 +374,8 @@
     def clear_tail(ref):
         for turn in range(2):
             for side in range(SIDES):
-                ref[turn, side, TRACE:ROWS, :] = jnp.zeros((ROWS - TRACE, E_DEV), jnp.float32)
+                for b in range(E_DEV // LANES):
+                    ref[turn, side, b, TRACE:ROWS, :] = jnp.zeros((ROWS - TRACE, LANES), jnp.float32)
 
     def complete_ghosts():
         for k in range(4):
@@ -377,13 +383,11 @@
             both = wide_dot(left, match[k])
             ghost_sum[k] = near_in[4 + k] + both[0:ROWS] + both[ROWS:2 * ROWS]
 
-    def pick_back():
-        both = wide_dot(stacked([near_in[k] for k in range(4)]), hot_back[...])
-        for side in range(SIDES):
-            for b in range(E_DEV // LANES):
-                first = side * E_DEV + b * LANES
-                part = both[0:ROWS, first:first + LANES] + both[ROWS:2 * ROWS, first:first + LANES]
-                picked1[side, b] = picked1[side, b] + part
+    def pick_back(b):
+        both = wide_dot(back_left[...], hot_back[b])
+        for side in range(SIDES):
+            cols = slice(side * LANES, (side + 1) * LANES)
+            picked1[side, b] = picked1[side, b] + both[0:ROWS, cols] + both[ROWS:2 * ROWS, cols]
 
     lists = [jnp.where(alive[k][0:1], share_ref[k:k + 1, :].astype(jnp.float32), -1.0) for k in range(4)]
     for k in range(4):
@@ -393,8 +397,8 @@
     clear_tail(product)
     for side in range(SIDES):
         for b in range(E_DEV // LANES):
-            first = side * E_DEV + b * LANES
-            hot[first:first + LANES, :] = one_hot_low(map_ref[side:side + 1, b * LANES:(b + 1) * LANES])
+            first = side * LANES
+            hot[b, first:first + LANES, :] = one_hot_low(map_ref[side:side + 1, b * LANES:(b + 1) * LANES])
     for k in range(4):
         hot_share[k * GH:(k + 1) * GH, :] = one_hot_low(share_ref[k:k + 1, :])
     square, weighted = face_sums(field0)
@@ -404,8 +408,8 @@
             for b in range(E_DEV // LANES):
                 cols = slice(b * LANES, (b + 1) * LANES)
                 hit = column == map_ref[side:side + 1, cols].astype(jnp.float32)
-                first = side * E_DEV + b * LANES
-                hot_back[u * GH:(u + 1) * GH, first:first + LANES] = jnp.where(hit, 1.0, 0.0).astype(jnp.bfloat16)
+                first = side * LANES
+                hot_back[b, u * GH:(u + 1) * GH, first:first + LANES] = jnp.where(hit, 1.0, 0.0).astype(jnp.bfloat16)
     pl.semaphore_wait(meet_sem.at[0], 3)
     meet(1, line_z)
     matrix_copy.wait()
@@ -422,9 +426,13 @@
     trade_wait_recv(0)
     lists_wait(list_recv, near_from)
 
-    pick_ghost(ghost_in, picked0)
-    multiply(0, picked0)
-    scatter_ghost(0)
+    total = None
+    for b in range(E_DEV // LANES):
+        pick_ghost(ghost_in, picked0, b)
+        multiply(0, picked0, b)
+        part = scatter_block(0, (4, 5), b)
+        total = part if total is None else total + part
+    scatter_ghost(0, total)
     send_cross()
     send_part(0)
     scatter_own(0, field0)
@@ -438,12 +446,22 @@
             match[k, u * GH:(u + 1) * GH, :] = jnp.where(hit, 1.0, 0.0).astype(jnp.bfloat16)
     trade_wait_recv(1)
     complete_ghosts()
-    pick_back()
+    back_left[...] = stacked([near_in[k] for k in range(4)])
+    pick_back(0)
+    pick_ghost(ghost_sum, picked1, 0)
     add_back(0, near_in)
-    pick_ghost(ghost_sum, picked1)
-    multiply(1, picked1)
+    last = E_DEV // LANES - 1
+
+    def middle(b, carry):
+        multiply(1, picked1, b)
+        pick_back(b + 1)
+        pick_ghost(ghost_sum, picked1, b + 1)
+        return carry
+
+    lax.fori_loop(0, last, middle, 0)
     norm0, curve0 = sum_finish(0)
     step0 = norm0 / curve0
+    multiply(1, picked1, last)
     for b in range(F_DEV // LANES):
         cols = slice(b * LANES, (b + 1) * LANES)
         field1[:, cols] = field0[:, cols] - step0 * image[0, :, cols]
@@ -502,10 +520,11 @@
             pltpu.VMEM((8, LANES), f32),
             pltpu.VMEM((SIDES, 4, ROWS, LANES), f32),
             pltpu.VMEM((SIDES, 4, ROWS, LANES), f32),
-            pltpu.VMEM((2, SIDES, ROWS, E_DEV), f32),
-            pltpu.VMEM((SIDES * E_DEV, WIDE), bf16),
+            pltpu.VMEM((2, SIDES, E_DEV // LANES, ROWS, LANES), f32),
+            pltpu.VMEM((E_DEV // LANES, SIDES * LANES, WIDE), bf16),
             pltpu.VMEM((4 * GH, WIDE), bf16),
-            pltpu.VMEM((4 * GH, SIDES * E_DEV), bf16),
+            pltpu.VMEM((E_DEV // LANES, 4 * GH, SIDES * LANES), bf16),
+            pltpu.VMEM((2 * ROWS, 4 * GH), bf16),
             pltpu.VMEM((4, 4 * GH, GH), bf16),
             pltpu.VMEM((2, 4, ROWS, GH), f32),
             pltpu.VMEM((4, ROWS, GH), f32),
@@ -516,7 +535,7 @@
             pltpu.VMEM((4, GH), f32),
             pltpu.VMEM((4, 4, GH), f32),
             pltpu.VMEM((2, 1, LANES), f32),
-            pltpu.VMEM((2, N_DOM, 1, LANES), f32),
+            pltpu.VMEM((2, N_DOM, LANES), f32),
             pltpu.SemaphoreType.DMA,
             pltpu.SemaphoreType.DMA((3,)),
             pltpu.SemaphoreType.DMA((3,)),

time: 28.9 us -> 28 us (0.969)
  Pallas kernels: 27.5 us -> 26.6 us
    pallas_call x1, Pallas kernels: 27.5 us -> 26.6 us  [shards(): pl.pallas_call(kernel, name='trace_cg', out_shape=(out, out, out, out), i...]
where the time goes in v6:
time: 28 us; the launch traced here: 27.9 us
  Pallas kernels  26.6 us (95%)
  other arithmetic  0.7 us (2%)
  between operations  0.64 us (2%)
    pallas_call x1, Pallas kernels, shards(): pl.pallas_call(kernel, name='trace_cg', out_shape=(out, out, out, out), i...  26.6 us
    sub x1, other arithmetic, shards(): return (lead + step * later, later - step * along)  0.7 us

profile of v6, /device:TPU:1, one launch (start us, length us, event | category | flops | bytes accessed | tf_op | source)
XLA Modules:
  0.0 27.9 jit_solution(10642117842769187477)
XLA Ops:
  0.6 26.6 %trace_cg.1 = (f32[18,1024]{1,0:T(8,128)S(1)}, f32[18,1024]{1,0:T(8,128)S(1)}, f32[18,1024]{1,0:T(8,128)S(1)}, f32[18,1024]{1,0:T(8,128)S(1)}) custom-call(f32[18,1024]{1,0:T(8,128)} %right_hbm.1, bf16[72,72,512]{2,1,0:T(8,128)(2,1)} %matrix_hbm.1, s32[4,512]{1,0:T(4,128)} %map_hbm.1, s32[4,128]{1,0:T(4,128)} %bitcast.7, s32[1,4]{1,0:T(1,128)} %count_hbm.1, ...), custom_call_target="tpu_custom_call" | custom-call | tf_op jit(solution)/shard_map/trace_cg/pallas_call | solution.py:499
  27.2 0.7 %multiply_subtract_fusion = (f32[18,1024]{1,0:T(8,128)}, f32[18,1024]{1,0:T(8,128)}) fusion(f32[18,1024]{1,0:T(8,128)S(1)} %get-tuple-element.8, f32[18,1024]{1,0:T(8,128)S(1)} %get-tuple-element.7, f32[18,1024]{1,0:T(8,128)S(1)} %get-tuple-element.9, f32[18,1024]{1,0:T(8,128)S(1)} %get-tuple-element.6), kind=kLoop, calls=%fused_computation | loop fusion | flops 73728 | bytes 442368 | tf_op jit(solution)/shard_map/sub | solution.py:554

commit v7 on v6

--- a/solution.py
+++ b/solution.py
@@ -77,10 +77,51 @@
     lead_ref, later_ref, along_ref, step_ref,
     right_ref, map_ref, share_ref, count_ref, mass_ref, absorb_ref, imped_ref, load_sem, meet_sem,
     matrix, widened, field0, field1, image, diag, picked0, picked1, product, hot, hot_share, hot_back, back_left, match,
-    out_buf, ghost_in, part_buf, back_in, near_in, ghost_sum, list_out, list_in, sum_buf, sum_in,
-    matrix_sem, trade_send, trade_recv, list_send, list_recv, sum_send, sum_recv,
+    out_buf, ghost_in, part_buf, back_in, near_in, ghost_sum, sum_buf, sum_in,
+    matrix_sem, trade_send, trade_recv, sum_send, sum_recv,
 ):
     me = lax.axis_index("dom")
+    rows18, rows22 = pl.ds(0, TRACE), pl.ds(0, TRACE + 4)
+
+    def blocks_wait(ref, rows, sem, count, options):
+        for n in options:
+            @pl.when(count == n)
+            def _(n=n):
+                some = ref.at[pl.ds(0, n), rows]
+                pltpu.make_async_copy(some, some, sem).wait()
+
+    core = lax.rem(me, 2)
+    at_x = lax.rem(me // 2, 4)
+    at_y = lax.rem(me // 8, 4)
+    at_z = me // 32
+
+    along_x = [lax.rem(at_x + d, 4) * 2 for d in range(4)]
+    along_y = [lax.rem(at_y + d, 4) * 8 for d in range(4)]
+    along_z = [lax.rem(at_z + d, 4) * 32 for d in range(4)]
+    cores = (core, 1 - core)
+
+    def device_at(dz, dy, dx, dc):
+        return along_z[dz] + along_y[dy] + along_x[dx] + cores[dc]
+
+    inside_to = [(me + o >= 0) & (me + o < N_DOM) for o in OFFSETS]
+    inside_from = [(me - o >= 0) & (me - o < N_DOM) for o in OFFSETS]
+    crosses = sorted(
+        ((k, u) for k in range(4) for u in range(4) if k != u), key=lambda at: -abs(OFFSETS[at[1]] - OFFSETS[at[0]])
+    )
+
+    def cross_ok(k, u):
+        user = me - OFFSETS[k] + OFFSETS[u]
+        return inside_from[k] & (user >= 0) & (user < N_DOM)
+
+
+    def tally(flags):
+        return functools.reduce(lambda total, flag: total + flag.astype(jnp.int32), flags, jnp.int32(0))
+
+    barrier = pltpu.get_barrier_semaphore()
+    for k, o in sorted(enumerate(OFFSETS), key=lambda at: -abs(at[1])):
+        @pl.when(inside_to[k])
+        def _():
+            pl.semaphore_signal(barrier, inc=1, device_id=(me + o,), device_id_type=MESH)
     loads = [
         pltpu.make_async_copy(source, target, load_sem.at[at])
         for at, (source, target) in enumerate((
@@ -88,93 +129,32 @@
             (mass_hbm, mass_ref), (absorb_hbm, absorb_ref), (imped_hbm, imped_ref),
         ))
     ]
-    rows18 = pl.ds(0, TRACE)
-
-    def blocks_wait(ref, sem, count, options):
-        for n in options:
-            @pl.when(count == n)
-            def _(n=n):
-                some = ref.at[pl.ds(0, n), rows18]
-                pltpu.make_async_copy(some, some, sem).wait()
-
-    core = lax.rem(me, 2)
-    at_x = lax.rem(me // 2, 4)
-    at_y = lax.rem(me // 8, 4)
-    at_z = me // 32
-
-    along_x = [lax.rem(at_x + d, 4) * 2 for d in range(4)]
-    along_y = [lax.rem(at_y + d, 4) * 8 for d in range(4)]
-    along_z = [lax.rem(at_z + d, 4) * 32 for d in range(4)]
-    cores = (core, 1 - core)
-
-    def device_at(dz, dy, dx, dc):
-        return along_z[dz] + along_y[dy] + along_x[dx] + cores[dc]
-
-    inside_to = [(me + o >= 0) & (me + o < N_DOM) for o in OFFSETS]
-    inside_from = [(me - o >= 0) & (me - o < N_DOM) for o in OFFSETS]
-    crosses = sorted(
-        ((k, u) for k in range(4) for u in range(4) if k != u), key=lambda at: -abs(OFFSETS[at[1]] - OFFSETS[at[0]])
-    )
-
-    def cross_ok(k, u):
-        user = me - OFFSETS[k] + OFFSETS[u]
-        return inside_from[k] & (user >= 0) & (user < N_DOM)
-
-
-    def tally(flags):
-        return functools.reduce(lambda total, flag: total + flag.astype(jnp.int32), flags, jnp.int32(0))
-
-    near_to, near_from = tally(inside_to), tally(inside_from)
-    all_near = near_to + near_from + tally([cross_ok(k, u) for k, u in crosses])
-
-    barrier = pltpu.get_barrier_semaphore()
-    arrivals = jnp.int32(13)
-    for k, o in enumerate(OFFSETS):
-        @pl.when(inside_to[k])
-        def _():
-            pl.semaphore_signal(barrier, inc=1, device_id=(me + o,), device_id_type=MESH)
-        arrivals = arrivals + inside_from[k].astype(jnp.int32)
+    for load in loads[:4]:
+        load.start()
+    for load in loads[4:]:
+        load.start()
+    matrix_copy = pltpu.make_async_copy(matrix_hbm, matrix, matrix_sem)
+    matrix_copy.start()
+
     line_y = [device_at(0, d, 0, 0) for d in range(1, 4)]
     line_z = [device_at(d, 0, 0, 0) for d in range(1, 4)]
     pairs_x = [device_at(0, 0, d, c) for d in range(4) for c in range(2) if d or c]
     for other in pairs_x + line_y + line_z:
         pl.semaphore_signal(barrier, inc=1, device_id=(other,), device_id_type=MESH)
 
-    for load in loads:
-        load.start()
-    matrix_copy = pltpu.make_async_copy(matrix_hbm, matrix, matrix_sem)
-    matrix_copy.start()
-
+    near_to, near_from = tally(inside_to), tally(inside_from)
+    all_near = near_to + near_from + tally([cross_ok(k, u) for k, u in crosses])
+
+    arrivals = 13 + near_from
 
     def meet(at, others):
         for other in others:
             pl.semaphore_signal(meet_sem.at[at], inc=1, device_id=(other,), device_id_type=MESH)
 
-    for load in loads:
+    for load in loads[:3]:
         load.wait()
     field0[0:TRACE, :] = right_ref[...]
     field0[TRACE:ROWS, :] = jnp.zeros((ROWS - TRACE, F_DEV), jnp.float32)
-    diag[...] = mass_ref[...] + absorb_ref[...].astype(jnp.float32) * imped_ref[...]
-    blank = jnp.zeros((TRACE, GH), jnp.float32)
-    for k in range(4):
-        @pl.when(jnp.logical_not(inside_from[k]))
-        def _():
-            ghost_in[k, 0:TRACE] = blank
-            near_in[4 + k, 0:TRACE] = blank
-            list_in[k] = jnp.full((4, GH), -1.0, jnp.float32)
-        @pl.when(jnp.logical_not(inside_to[k]))
-        def _():
-            near_in[k, 0:TRACE] = blank
-            back_in[k, 0:TRACE] = blank
-        for ref in (ghost_in, back_in):
-            ref[k, TRACE:ROWS] = jnp.zeros((ROWS - TRACE, GH), jnp.float32)
-    for k, u in crosses:
-        @pl.when(jnp.logical_not(cross_ok(k, u)))
-        def _():
-            near_in[8 + 4 * k + u, 0:TRACE] = blank
-    for at in range(24):
-        near_in[at, TRACE:ROWS] = jnp.zeros((ROWS - TRACE, GH), jnp.float32)
-
     lane = lax.broadcasted_iota(jnp.int32, (ROWS, GH), 1)
     alive = [lane < count_ref[0, k] for k in range(4)]
 
@@ -184,26 +164,14 @@
         ]
 
     def trade(turn, source, target, other):
+        rows = rows22 if turn == 0 else rows18
         return pltpu.make_async_remote_copy(
-            src_ref=source.at[rows18], dst_ref=target.at[rows18],
+            src_ref=source.at[rows], dst_ref=target.at[rows],
             send_sem=trade_send.at[turn], recv_sem=trade_recv.at[turn], device_id=(other,), device_id_type=MESH,
         )
 
     def out_copy(turn, k):
         return trade(turn, out_buf.at[turn, k], ghost_in.at[k] if turn == 0 else near_in.at[4 + k], me + OFFSETS[k])
-
-    def list_copy(k):
-        return pltpu.make_async_remote_copy(
-            src_ref=list_out, dst_ref=list_in.at[k], send_sem=list_send, recv_sem=list_recv,
-            device_id=(me + OFFSETS[k],), device_id_type=MESH,
-        )
-
-    def lists_wait(sem, count):
-        for n in (2, 3, 4):
-            @pl.when(count == n)
-            def _(n=n):
-                some = list_in.at[pl.ds(0, n)]
-                pltpu.make_async_copy(some, some, sem).wait()
 
     def cross_copy(k, u):
         return trade(1, part_buf.at[0, k], near_in.at[8 + 4 * u + k], me - OFFSETS[k] + OFFSETS[u])
@@ -219,25 +187,23 @@
 
     def trade_wait_recv(turn):
         ref, _, count, options = trades[turn]
-        blocks_wait(ref, trade_recv.at[turn], count, options)
+        blocks_wait(ref, rows18 if turn else rows22, trade_recv.at[turn], count, options)
 
     def trade_wait_send(turn):
         ref, count, _, options = trades[turn]
-        blocks_wait(ref, trade_send.at[turn], count, options)
+        blocks_wait(ref, rows18 if turn else rows22, trade_send.at[turn], count, options)
 
     def send_out(turn, ref):
         blocks = own_blocks(ref)
         for k in range(4):
             gone = lane_pick(blocks, share_ref[k:k + 1, :], 0, None)
-            out_buf[turn, k] = jnp.where(alive[k], gone, 0.0)
+            out_buf[turn, k, 0:TRACE] = jnp.where(alive[k], gone, 0.0)[0:TRACE]
         if turn == 0:
             pl.semaphore_wait(barrier, arrivals)
         for k in (0, 3, 1, 2):
             @pl.when(inside_to[k])
             def _():
                 out_copy(turn, k).start()
-                if turn == 0:
-                    list_copy(k).start()
 
     def send_part(turn):
         for k in range(4):
@@ -278,6 +244,22 @@
             total = one(side, total)
         for side in range(SIDES):
             product[turn, side, b, 0:TRACE, :] = total[side * TRACE:(side + 1) * TRACE]
+
+    def scatter_block(turn, groups, b):
+        lefts = [
+            spread_rows(product[turn, side, b], map_ref[side:side + 1, b * LANES:(b + 1) * LANES], groups)
+            for side in range(SIDES)
+        ]
+        return wide_dot(jnp.concatenate(lefts, axis=1), hot[b])
+
+    def energy(step):
+        total = jnp.zeros((ROWS, LANES), jnp.float32)
+        for side in range(SIDES):
+            for b in range(E_DEV // LANES):
+                image_part = product[0, side, b] - step * product[1, side, b]
+                product[1, side, b] = image_part
+                total = total + (picked0[side, b] - step * picked1[side, b]) * image_part
+        return jnp.sum(total, axis=0, keepdims=True)
 
     def scatter_block(turn, groups, b):
         lefts = [
@@ -391,8 +373,31 @@
 
     lists = [jnp.where(alive[k][0:1], share_ref[k:k + 1, :].astype(jnp.float32), -1.0) for k in range(4)]
     for k in range(4):
-        list_out[k:k + 1, :] = lists[k]
+        out_buf[0, k, TRACE:TRACE + 4] = jnp.concatenate(lists, axis=0)
     send_out(0, field0)
+    for load in loads[3:]:
+        load.wait()
+    diag[...] = mass_ref[...] + absorb_ref[...].astype(jnp.float32) * imped_ref[...]
+    blank = jnp.zeros((TRACE, GH), jnp.float32)
+    for k in range(4):
+        @pl.when(jnp.logical_not(inside_from[k]))
+        def _():
+            ghost_in[k, 0:TRACE] = blank
+            near_in[4 + k, 0:TRACE] = blank
+            ghost_in[k, TRACE:TRACE + 4] = jnp.full((4, GH), -1.0, jnp.float32)
+        @pl.when(jnp.logical_not(inside_to[k]))
+        def _():
+            near_in[k, 0:TRACE] = blank
+            back_in[k, 0:TRACE] = blank
+        ghost_in[k, TRACE + 4:ROWS] = jnp.zeros((ROWS - TRACE - 4, GH), jnp.float32)
+        back_in[k, TRACE:ROWS] = jnp.zeros((ROWS - TRACE, GH), jnp.float32)
+    for k, u in crosses:
+        @pl.when(jnp.logical_not(cross_ok(k, u)))
+        def _():
+            near_in[8 + 4 * k + u, 0:TRACE] = blank
+    for at in range(24):
+        near_in[at, TRACE:ROWS] = jnp.zeros((ROWS - TRACE, GH), jnp.float32)
+
     meet(0, line_y)
     clear_tail(product)
     for side in range(SIDES):
@@ -424,25 +429,28 @@
     lax.fori_loop(0, DOFS, widen, 0, unroll=2)
     pl.semaphore_wait(meet_sem.at[1], 3)
     trade_wait_recv(0)
-    lists_wait(list_recv, near_from)
-
-    total = None
+
+    total, force = None, None
     for b in range(E_DEV // LANES):
         pick_ghost(ghost_in, picked0, b)
         multiply(0, picked0, b)
         part = scatter_block(0, (4, 5), b)
         total = part if total is None else total + part
+        for side in range(SIDES):
+            both = picked0[side, b] * product[0, side, b]
+            force = both if force is None else force + both
     scatter_ghost(0, total)
     send_cross()
     send_part(0)
     scatter_own(0, field0)
     send_out(1, image.at[0])
-    sum_start(0, square, weighted + energy(None))
+    sum_start(0, square, weighted + jnp.sum(force, axis=0, keepdims=True))
     pick_own(image.at[0], picked1)
     for k in range(4):
-        target = jnp.where(list_in[k, k:k + 1, :] < 0.0, -2.0, list_in[k, k:k + 1, :])
+        mine = ghost_in[k, TRACE + k:TRACE + k + 1, :]
+        target = jnp.where(mine < 0.0, -2.0, mine)
         for u in range(4):
-            hit = as_column(list_in[k, u:u + 1, :]) == target
+            hit = as_column(ghost_in[k, TRACE + u:TRACE + u + 1, :]) == target
             match[k, u * GH:(u + 1) * GH, :] = jnp.where(hit, 1.0, 0.0).astype(jnp.bfloat16)
     trade_wait_recv(1)
     complete_ghosts()
@@ -485,7 +493,6 @@
 
     for turn in range(3):
         trade_wait_send(turn)
-    lists_wait(list_send, near_to)
     pltpu.make_async_copy(
         sum_in.at[:, pl.ds(0, N_DOM - 1)], sum_in.at[:, pl.ds(1, N_DOM - 1)], sum_send
     ).wait()
@@ -532,15 +539,11 @@
             pltpu.VMEM((4, ROWS, GH), f32),
             pltpu.VMEM((24, ROWS, GH), f32),
             pltpu.VMEM((4, ROWS, GH), f32),
-            pltpu.VMEM((4, GH), f32),
-            pltpu.VMEM((4, 4, GH), f32),
             pltpu.VMEM((2, 1, LANES), f32),
             pltpu.VMEM((2, N_DOM, LANES), f32),
             pltpu.SemaphoreType.DMA,
             pltpu.SemaphoreType.DMA((3,)),
             pltpu.SemaphoreType.DMA((3,)),
-            pltpu.SemaphoreType.DMA,
-            pltpu.SemaphoreType.DMA,
             pltpu.SemaphoreType.DMA,
             pltpu.SemaphoreType.DMA((2,)),
         ],

time: 28 us -> 28 us (level)
  no operation moved by 1% of the time
where the time goes in v7:
time: 28 us; the launch traced here: 27.9 us
  Pallas kernels  26.5 us (95%)
  other arithmetic  0.7 us (2%)
  between operations  0.64 us (2%)
    pallas_call x1, Pallas kernels, shards(): pl.pallas_call(kernel, name='trace_cg', out_shape=(out, out, out, out), i...  26.5 us
    sub x1, other arithmetic, shards(): return (lead + step * later, later - step * along)  0.7 us

profile of v7, /device:TPU:1, one launch (start us, length us, event | category | flops | bytes accessed | tf_op | source)
XLA Modules:
  0.0 27.9 jit_solution(9647335604782827053)
XLA Ops:
  0.6 26.5 %trace_cg.1 = (f32[18,1024]{1,0:T(8,128)S(1)}, f32[18,1024]{1,0:T(8,128)S(1)}, f32[18,1024]{1,0:T(8,128)S(1)}, f32[18,1024]{1,0:T(8,128)S(1)}) custom-call(f32[18,1024]{1,0:T(8,128)} %right_hbm.1, bf16[72,72,512]{2,1,0:T(8,128)(2,1)} %matrix_hbm.1, s32[4,512]{1,0:T(4,128)} %map_hbm.1, s32[4,128]{1,0:T(4,128)} %bitcast.7, s32[1,4]{1,0:T(1,128)} %count_hbm.1, ...), custom_call_target="tpu_custom_call" | custom-call | tf_op jit(solution)/shard_map/trace_cg/pallas_call | solution.py:506
  27.2 0.7 %multiply_subtract_fusion = (f32[18,1024]{1,0:T(8,128)}, f32[18,1024]{1,0:T(8,128)}) fusion(f32[18,1024]{1,0:T(8,128)S(1)} %get-tuple-element.8, f32[18,1024]{1,0:T(8,128)S(1)} %get-tuple-element.7, f32[18,1024]{1,0:T(8,128)S(1)} %get-tuple-element.9, f32[18,1024]{1,0:T(8,128)S(1)} %get-tuple-element.6), kind=kLoop, calls=%fused_computation | loop fusion | flops 73728 | bytes 442368 | tf_op jit(solution)/shard_map/sub | solution.py:557

commit v8 on v7

--- a/solution.py
+++ b/solution.py
@@ -123,7 +123,7 @@
         def _():
             pl.semaphore_signal(barrier, inc=1, device_id=(me + o,), device_id_type=MESH)
     loads = [
-        pltpu.make_async_copy(source, target, load_sem.at[at])
+        pltpu.make_async_copy(source, target, load_sem.at[min(at, 4)])
         for at, (source, target) in enumerate((
             (share_hbm, share_ref), (count_hbm, count_ref), (right_hbm, right_ref), (map_hbm, map_ref),
             (mass_hbm, mass_ref), (absorb_hbm, absorb_ref), (imped_hbm, imped_ref),
@@ -375,8 +375,8 @@
     for k in range(4):
         out_buf[0, k, TRACE:TRACE + 4] = jnp.concatenate(lists, axis=0)
     send_out(0, field0)
-    for load in loads[3:]:
-        load.wait()
+    loads[3].wait()
+    pltpu.make_async_copy(near_in.at[0], near_in.at[0], load_sem.at[4]).wait()
     diag[...] = mass_ref[...] + absorb_ref[...].astype(jnp.float32) * imped_ref[...]
     blank = jnp.zeros((TRACE, GH), jnp.float32)
     for k in range(4):
@@ -480,6 +480,9 @@
     scatter_own(1, field1)
     trade_wait_recv(2)
     add_back(1, back_in)
+    for b in range(F_DEV // LANES):
+        cols = slice(b * LANES, (b + 1) * LANES)
+        later_ref[:, cols] = field1[0:TRACE, cols]
     norm1, curve1 = sum_finish(1)
     ratio = norm1 / norm0
     step1 = norm1 / (curve1 - ratio * norm1 / step0)
@@ -487,7 +490,6 @@
     for b in range(F_DEV // LANES):
         cols = slice(b * LANES, (b + 1) * LANES)
         lead_ref[:, cols] = lead * field0[0:TRACE, cols]
-        later_ref[:, cols] = field1[0:TRACE, cols]
         along_ref[:, cols] = image[1, 0:TRACE, cols] + ratio * image[0, 0:TRACE, cols]
     step_ref[...] = jnp.broadcast_to(step1, (TRACE, F_DEV))
 
@@ -517,7 +519,7 @@
             pltpu.VMEM((8, LANES), f32),
             pltpu.VMEM((8, LANES), i32),
             pltpu.VMEM((8, LANES), f32),
-            pltpu.SemaphoreType.DMA((7,)),
+            pltpu.SemaphoreType.DMA((5,)),
             pltpu.SemaphoreType.REGULAR((2,)),
             pltpu.VMEM((DOFS, DOFS, E_DEV), bf16),
             pltpu.VMEM((E_DEV // LANES, DOFS, DOFS, LANES), f32),

time: 28 us -> 28 us (level)
  no operation moved by 1% of the time
where the time goes in v8:
time: 28 us; the launch traced here: 27.8 us
  Pallas kernels  26.5 us (95%)
  other arithmetic  0.7 us (2%)
  between operations  0.64 us (2%)
    pallas_call x1, Pallas kernels, shards(): pl.pallas_call(kernel, name='trace_cg', out_shape=(out, out, out, out), i...  26.5 us
    sub x1, other arithmetic, shards(): return (lead + step * later, later - step * along)  0.7 us

profile of v8, /device:TPU:1, one launch (start us, length us, event | category | flops | bytes accessed | tf_op | source)
XLA Modules:
  0.0 27.8 jit_solution(8571406870495517555)
XLA Ops:
  0.6 26.5 %trace_cg.1 = (f32[18,1024]{1,0:T(8,128)S(1)}, f32[18,1024]{1,0:T(8,128)S(1)}, f32[18,1024]{1,0:T(8,128)S(1)}, f32[18,1024]{1,0:T(8,128)S(1)}) custom-call(f32[18,1024]{1,0:T(8,128)} %right_hbm.1, bf16[72,72,512]{2,1,0:T(8,128)(2,1)} %matrix_hbm.1, s32[4,512]{1,0:T(4,128)} %map_hbm.1, s32[4,128]{1,0:T(4,128)} %bitcast.7, s32[1,4]{1,0:T(1,128)} %count_hbm.1, ...), custom_call_target="tpu_custom_call" | custom-call | tf_op jit(solution)/shard_map/trace_cg/pallas_call | solution.py:508
  27.1 0.7 %multiply_subtract_fusion = (f32[18,1024]{1,0:T(8,128)}, f32[18,1024]{1,0:T(8,128)}) fusion(f32[18,1024]{1,0:T(8,128)S(1)} %get-tuple-element.8, f32[18,1024]{1,0:T(8,128)S(1)} %get-tuple-element.7, f32[18,1024]{1,0:T(8,128)S(1)} %get-tuple-element.9, f32[18,1024]{1,0:T(8,128)S(1)} %get-tuple-element.6), kind=kLoop, calls=%fused_computation | loop fusion | flops 73728 | bytes 442368 | tf_op jit(solution)/shard_map/sub | solution.py:559

commit v9 on v8

--- a/solution.py
+++ b/solution.py
@@ -206,7 +206,7 @@
                 out_copy(turn, k).start()
 
     def send_part(turn):
-        for k in range(4):
+        for k in (0, 3, 1, 2):
             @pl.when(inside_from[k])
             def _():
                 part_copy(turn, k).start()
@@ -440,8 +440,8 @@
             both = picked0[side, b] * product[0, side, b]
             force = both if force is None else force + both
     scatter_ghost(0, total)
+    send_part(0)
     send_cross()
-    send_part(0)
     scatter_own(0, field0)
     send_out(1, image.at[0])
     sum_start(0, square, weighted + jnp.sum(force, axis=0, keepdims=True))

time: 28 us -> 27.9 us (level)
  no operation moved by 1% of the time
where the time goes in v9:
time: 27.9 us; the launch traced here: 27.8 us
  Pallas kernels  26.5 us (95%)
  other arithmetic  0.7 us (3%)
  between operations  0.64 us (2%)
    pallas_call x1, Pallas kernels, shards(): pl.pallas_call(kernel, name='trace_cg', out_shape=(out, out, out, out), i...  26.5 us
    sub x1, other arithmetic, shards(): return (lead + step * later, later - step * along)  0.7 us

profile of v9, /device:TPU:1, one launch (start us, length us, event | category | flops | bytes accessed | tf_op | source)
XLA Modules:
  0.0 27.8 jit_solution(12321743637834077444)
XLA Ops:
  0.6 26.5 %trace_cg.1 = (f32[18,1024]{1,0:T(8,128)S(1)}, f32[18,1024]{1,0:T(8,128)S(1)}, f32[18,1024]{1,0:T(8,128)S(1)}, f32[18,1024]{1,0:T(8,128)S(1)}) custom-call(f32[18,1024]{1,0:T(8,128)} %right_hbm.1, bf16[72,72,512]{2,1,0:T(8,128)(2,1)} %matrix_hbm.1, s32[4,512]{1,0:T(4,128)} %map_hbm.1, s32[4,128]{1,0:T(4,128)} %bitcast.7, s32[1,4]{1,0:T(1,128)} %count_hbm.1, ...), custom_call_target="tpu_custom_call" | custom-call | tf_op jit(solution)/shard_map/trace_cg/pallas_call | solution.py:508
  27.1 0.7 %multiply_subtract_fusion = (f32[18,1024]{1,0:T(8,128)}, f32[18,1024]{1,0:T(8,128)}) fusion(f32[18,1024]{1,0:T(8,128)S(1)} %get-tuple-element.8, f32[18,1024]{1,0:T(8,128)S(1)} %get-tuple-element.7, f32[18,1024]{1,0:T(8,128)S(1)} %get-tuple-element.9, f32[18,1024]{1,0:T(8,128)S(1)} %get-tuple-element.6), kind=kLoop, calls=%fused_computation | loop fusion | flops 73728 | bytes 442368 | tf_op jit(solution)/shard_map/sub | solution.py:559
